TPU v7x, 32 devices: a 4x4x1 block of a 4x4x8 slice. The times are simulated.
32 devices in a mesh: data: 1 (over z), wg: 32 (over y, x, core).
Axes of the slice: x: 4, y: 4, z: 1, core: 2. Of those that a mesh axis runs over, the one named last changes fastest.
The devices are a block of a 4x4x8 slice.
Arguments:
- h0: bfloat16 [64, 512, 3072], P(('data', 'wg'))
- positions: int32 [64, 512], P(('data', 'wg'))
- norm_attn: float32 [1, 3072], replicated
- norm_mlp: float32 [1, 3072], replicated
- w_query: bfloat16 [1, 3072, 24, 128], P(None, 'wg')
- w_key: bfloat16 [1, 3072, 8, 128], P(None, 'wg')
- w_value: bfloat16 [1, 3072, 8, 128], P(None, 'wg')
- w_out: bfloat16 [1, 3072, 3072], P(None, 'wg')
- w_gate: bfloat16 [1, 3072, 8192], P(None, 'wg')
- w_up: bfloat16 [1, 3072, 8192], P(None, 'wg')
- w_down: bfloat16 [1, 8192, 3072], P(None, 'wg')
- norm_final: float32 [3072], replicated
Outputs:
- output: bfloat16 [64, 512, 3072], P(('data', 'wg'))
All inputs are finite; a program needn't handle non-finite values.
Results may differ from a plain program's by a relative error of at most 0.0172752.
Values are sent between devices in bfloat16 or wider.
A program may use at most 768 MiB of HBM per device.

v0:
```python
import jax
import jax.numpy as jnp
from jax import lax
from jax.sharding import PartitionSpec as P, NamedSharding

EPS = 1e-5
ROPE_BASE = 10000.0


def rms_norm(values_in, gain_vec):
    as_f32 = values_in.astype(jnp.float32)
    mean_sq = jnp.mean(as_f32 * as_f32, axis=-1, keepdims=True)
    return (as_f32 * lax.rsqrt(mean_sq + EPS) * gain_vec).astype(jnp.bfloat16)


def rope_tables(positions, head_dim):
    half_dim = head_dim // 2
    exponents = jnp.arange(half_dim, dtype=jnp.float32) * (2.0 / head_dim)
    inv_freq = jnp.power(jnp.float32(ROPE_BASE), -exponents)
    angles = positions.astype(jnp.float32)[..., None] * inv_freq
    return jnp.cos(angles)[:, :, None, :], jnp.sin(angles)[:, :, None, :]


def apply_rope(proj, cos_table, sin_table):
    half_dim = proj.shape[-1] // 2
    as_f32 = proj.astype(jnp.float32)
    first_half = as_f32[..., :half_dim]
    second_half = as_f32[..., half_dim:]
    rotated = jnp.concatenate([first_half * cos_table - second_half * sin_table, second_half * cos_table + first_half * sin_table], axis=-1)
    return rotated.astype(jnp.bfloat16)


def causal_attention(query_proj, key_proj, value_proj):
    n_seq, seq_len, kv_heads, n_rep, head_dim = query_proj.shape
    q_block = min(seq_len, 256)
    n_blocks = seq_len // q_block
    score_scale = head_dim ** -0.5
    key_index = jnp.arange(seq_len)

    def one_block(block_idx):
        start_row = block_idx * q_block
        query_block = lax.dynamic_slice_in_dim(query_proj, start_row, q_block, axis=1)
        scores = jnp.einsum('bqgrd,bkgd->bgrqk', query_block, key_proj, preferred_element_type=jnp.float32) * score_scale
        query_index = start_row + jnp.arange(q_block)
        allowed = key_index[None, :] <= query_index[:, None]
        scores = jnp.where(allowed, scores, -1e30)
        attn_probs = jax.nn.softmax(scores, axis=-1).astype(jnp.bfloat16)
        block_out = jnp.einsum('bgrqk,bkgd->bqgrd', attn_probs, value_proj, preferred_element_type=jnp.float32)
        return block_out.astype(jnp.bfloat16)

    attended = lax.map(one_block, jnp.arange(n_blocks))
    return jnp.moveaxis(attended, 0, 1).reshape(n_seq, seq_len, kv_heads * n_rep * head_dim)


def decoder_layer(residual, cos_table, sin_table, gain_attn, gain_mlp, w_query, w_key, w_value, w_out, w_gate, w_up, w_down):
    n_seq, seq_len = residual.shape[0], residual.shape[1]
    n_heads, head_dim = w_query.shape[1], w_query.shape[2]
    kv_heads = w_key.shape[1]
    normed = rms_norm(residual, gain_attn)
    query_proj = jnp.einsum('btd,dhe->bthe', normed, w_query, preferred_element_type=jnp.float32).astype(jnp.bfloat16)
    key_proj = jnp.einsum('btd,dhe->bthe', normed, w_key, preferred_element_type=jnp.float32).astype(jnp.bfloat16)
    value_proj = jnp.einsum('btd,dhe->bthe', normed, w_value, preferred_element_type=jnp.float32).astype(jnp.bfloat16)
    query_proj = apply_rope(query_proj, cos_table, sin_table).reshape(n_seq, seq_len, kv_heads, n_heads // kv_heads, head_dim)
    key_proj = apply_rope(key_proj, cos_table, sin_table)
    attended = causal_attention(query_proj, key_proj, value_proj)
    attn_out = jnp.einsum('btn,nd->btd', attended, w_out, preferred_element_type=jnp.float32)
    residual = (residual.astype(jnp.float32) + attn_out).astype(jnp.bfloat16)
    normed = rms_norm(residual, gain_mlp)
    gate_proj = jnp.einsum('btd,df->btf', normed, w_gate, preferred_element_type=jnp.float32)
    up_proj = jnp.einsum('btd,df->btf', normed, w_up, preferred_element_type=jnp.float32)
    hidden = (jax.nn.silu(gate_proj) * up_proj).astype(jnp.bfloat16)
    down_proj = jnp.einsum('btf,fd->btd', hidden, w_down, preferred_element_type=jnp.float32)
    return (residual.astype(jnp.float32) + down_proj).astype(jnp.bfloat16)


def solution(mesh):
    token_spec = P(('data', 'wg'))
    weight_spec = P(None, 'wg')
    whole_spec = P()
    in_specs = (token_spec, token_spec, whole_spec, whole_spec, weight_spec, weight_spec, weight_spec, weight_spec, weight_spec, weight_spec, weight_spec, whole_spec)

    def local_forward(h0, positions, norm_attn, norm_mlp, w_query, w_key, w_value, w_out, w_gate, w_up, w_down, norm_final):
        cos_table, sin_table = rope_tables(positions, w_query.shape[-1])
        residual = h0
        for layer_idx in range(w_query.shape[0]):
            full_query = lax.all_gather(w_query[layer_idx], 'wg', axis=0, tiled=True)
            full_key = lax.all_gather(w_key[layer_idx], 'wg', axis=0, tiled=True)
            full_value = lax.all_gather(w_value[layer_idx], 'wg', axis=0, tiled=True)
            full_out = lax.all_gather(w_out[layer_idx], 'wg', axis=0, tiled=True)
            full_gate = lax.all_gather(w_gate[layer_idx], 'wg', axis=0, tiled=True)
            full_up = lax.all_gather(w_up[layer_idx], 'wg', axis=0, tiled=True)
            full_down = lax.all_gather(w_down[layer_idx], 'wg', axis=0, tiled=True)
            residual = decoder_layer(residual, cos_table, sin_table, norm_attn[layer_idx], norm_mlp[layer_idx], full_query, full_key, full_value, full_out, full_gate, full_up, full_down)
        return rms_norm(residual, norm_final)

    return jax.shard_map(local_forward, mesh=mesh, in_specs=in_specs, out_specs=token_spec, check_vma=False)
```

profile of v0, /device:TPU:97, one launch (start us, length us, event | category | flops | bytes accessed | tf_op | source)
XLA Modules:
  0.0 784.2 jit_solution(7999197966177913056)
XLA Ops:
  6.5 0.0 copy-start.4
  6.5 0.0 all-gather.17.cloned.1.call-start
  6.6 0.7 all-gather.17.cloned.1.call-update
  7.3 0.1 all-gather.19.cloned.1.call-start
  7.4 1.6 copy.33
  9.0 0.1 all-gather.19.cloned.1.call-update
  9.1 0.1 all-gather.15.cloned.1.call-start
  9.1 0.7 all-gather.15.cloned.1.call-update
  9.9 0.1 all-gather.21.cloned.1.call-start
  9.9 0.6 all-gather.21.cloned.1.call-update
  10.5 0.1 all-gather.23.cloned.1.call-start
  10.6 0.6 all-gather.23.cloned.1.call-update
  11.2 0.1 all-gather.25.cloned.1.call-start
  11.2 0.6 all-gather.25.cloned.1.call-update
  11.8 0.1 all-gather.27.cloned.1.call-start
  11.9 0.7 all-gather.27.cloned.1.call-update
  12.6 0.0 copy-done.4
  12.7 4.1 fusion.46
  16.7 1.0 multiply_cosine_fusion
  17.7 0.0 copy-start
  17.8 0.0 copy-start.5
  17.8 39.8 %all-gather.17.cloned.1.call-done = bf16[1,3072,8,128]{3,2,0,1:T(8,128)(2,1)} async-done(((bf16[1,96,8,128]{3,2,0,1:T(8,128)(2,1)}), bf16[1,3072,8,128]{3,2,0,1:T(8,128)(2,1)}) %all-gather.17.cloned.1.call-update) | async-done | bytes 6291472 | tf_op jit(solution)/shard_map/all_gather | solution.py:87
  57.5 9.0 %copy.32 = bf16[1,3072,8,128]{1,3,2,0:T(8,128)(2,1)} copy(bf16[1,3072,8,128]{3,2,0,1:T(8,128)(2,1)} %all-gather.17.cloned.1.call-done) | data formatting | bytes 12582912 | tf_op jit(solution)/shard_map/all_gather | solution.py:87
  66.5 0.0 copy-done.5
  66.5 10.8 %convert_convert_fusion.1 = f32[2,512,8,128]{1,3,2,0:T(8,128)S(1)} fusion(bf16[1,3072,8,128]{1,3,2,0:T(8,128)(2,1)} %copy.32, bf16[2,512,3072]{2,1,0:T(8,128)(2,1)} %param.14, f32[3072]{0:T(1024)S(1)} %bitcast.113, f32[2,512]{1,0:T(2,128)S(1)} %add_rsqrt_fusion.2), kind=kOutput, calls=%fused_computation.68 | convolution fusion | flops 6457131008 | bytes 16793600 | tf_op jit(solution)/shard_map/btd,dhe->bthe/dot_general | solution.py:61
  77.4 0.0 copy-done
  77.4 0.8 subtract_convert_fusion.1
  78.1 0.2 pad_maximum_fusion.1
  78.3 2.4 copy.34
  80.7 21.5 %all-gather.19.cloned.1.call-done = bf16[1,3072,8,128]{3,1,2,0:T(8,128)(2,1)} async-done(((bf16[1,96,8,128]{3,1,2,0:T(8,128)(2,1)}), bf16[1,3072,8,128]{3,1,2,0:T(8,128)(2,1)}) %all-gather.19.cloned.1.call-update) | async-done | bytes 6291472 | tf_op jit(solution)/shard_map/all_gather | solution.py:88
  102.2 11.7 %fusion.69 = bf16[2,512,8,128]{3,1,2,0:T(8,128)(2,1)} fusion(bf16[1,3072,8,128]{3,1,2,0:T(8,128)(2,1)} %all-gather.19.cloned.1.call-done, bf16[2,512,3072]{2,1,0:T(8,128)(2,1)} %param.14, f32[3072]{0:T(1024)S(1)} %bitcast.114, f32[2,512]{1,0:T(2,128)S(1)} %add_rsqrt_fusion.2), kind=kOutput, calls=%fused_computation.69 | convolution fusion | flops 6456082432 | bytes 14696448 | tf_op jit(solution)/shard_map/btd,dhe->bthe/dot_general | solution.py:62
  113.9 61.4 %all-gather.15.cloned.1.call-done = bf16[1,3072,24,128]{3,2,0,1:T(8,128)(2,1)} async-done(((bf16[1,96,24,128]{3,2,0,1:T(8,128)(2,1)}), bf16[1,3072,24,128]{3,2,0,1:T(8,128)(2,1)}) %all-gather.15.cloned.1.call-update) | async-done | bytes 18874384 | tf_op jit(solution)/shard_map/all_gather | solution.py:86
  175.3 24.1 %copy.28 = bf16[1,3072,24,128]{1,3,2,0:T(8,128)(2,1)} copy(bf16[1,3072,24,128]{3,2,0,1:T(8,128)(2,1)} %all-gather.15.cloned.1.call-done) | data formatting | bytes 37748736 | tf_op jit(solution)/shard_map/all_gather | solution.py:86
  199.4 0.0 copy-start.1
  199.4 25.4 %convert_convert_fusion = f32[2,512,24,128]{1,3,2,0:T(8,128)S(1)} fusion(bf16[1,3072,24,128]{1,3,2,0:T(8,128)(2,1)} %copy.28, bf16[2,512,3072]{2,1,0:T(8,128)(2,1)} %param.14, f32[3072]{0:T(1024)S(1)} %bitcast.115, f32[2,512]{1,0:T(2,128)S(1)} %add_rsqrt_fusion.2), kind=kOutput, calls=%fused_computation.64 | convolution fusion | flops 19346227200 | bytes 37765120 | tf_op jit(solution)/shard_map/btd,dhe->bthe/dot_general | solution.py:60
  224.8 0.0 copy-done.1
  224.8 3.5 subtract_convert_fusion
  228.3 6.6 copy.29
  234.8 4.6 copy.30
  239.4 0.0 copy-start.2
  239.4 9.8 %pad_maximum_fusion = bf16[2,512,8,3,128]{4,1,3,2,0:T(8,128)(2,1)} fusion(bf16[2,512,8,3,64]{4,1,3,2,0:T(8,128)(2,1)} %copy.30, bf16[2,512,8,3,64]{4,1,3,2,0:T(8,128)(2,1)} %copy.29), kind=kLoop, calls=%fused_computation.57 | loop fusion | flops 12582912 | bytes 12582912 | tf_op jit(solution)/shard_map/concatenate | solution.py:29
  249.2 0.0 copy-done.2
  249.2 58.2 %while.11 = (s32[]{:T(128)}, bf16[2,2,256,8,3,128]{5,2,4,3,1,0:T(8,128)(2,1)}, s32[2]{0:T(128)S(1)}, bf16[2,512,8,3,128]{4,1,3,2,0:T(8,128)(2,1)}, bf16[2,512,8,...) while((s32[]{:T(128)}, ...), condition=%wide.region_4.5_spmd.clone, body=%wide.region_1.4_spmd.clone.sunk | while | flops 3260678912 | bytes 61180584 | solution.py:51
  249.3 0.7 dynamic_slice.24
  250.6 0.1 iota_compare_fusion.2
  250.8 15.2 %fusion.99 = (f32[2,8,3,256]{3,2,1,0:T(4,128)S(1)}, f32[2,8,3,256,512]{4,3,2,1,0:T(8,128)}) fusion(pred[256,512]{1,0:T(8,128)(4,1)S(1)} %iota_compare_fusion.2, bf16[2,512,8,3,128]{4,1,3,2,0:T(8,128)(2,1)} %get-tuple-element.163, s32[]{:T(128)S(6)} %select_n.28, bf16[2,512,8,128]{3,1,2,0:T(8,128)(2,1)S(1)} %get-tuple-element.164), kind=kOutput, calls=%fused_computation.76.clone.1 | convolution fusion | flops 1635779072 | bytes 30588932 | tf_op jit(solution)/shard_map/while/body/eval_jaxpr/sub | solution.py:47
  266.0 12.4 %bitcast_dynamic-update-slice_fusion.2 = bf16[2,2,256,8,3,128]{5,2,4,3,1,0:T(8,128)(2,1)} fusion(bf16[2,2,256,8,3,128]{5,2,4,3,1,0:T(8,128)(2,1)} %get-tuple-element.151, s32[]{:T(128)} %get-tuple-element.150, f32[2,8,3,256,512]{4,3,2,1,0:T(8,128)} %get-tuple-element.138, f32[2,8,3,256]{3,2,1,0:T(4,128)S(1)} %get-tuple-element.139, ...), kind=kOutput, calls=%fused_computation.13.clone.1 | convolution fusion | flops 1624768512 | bytes 30458368 | tf_op jit(solution)/shard_map/while/body/eval_jaxpr/bgrqk,bkgd->bqgrd/dot_general | solution.py:48
  278.3 0.6 dynamic_slice.24
  279.6 0.1 iota_compare_fusion.2
  279.8 15.2 %fusion.99 = (f32[2,8,3,256]{3,2,1,0:T(4,128)S(1)}, f32[2,8,3,256,512]{4,3,2,1,0:T(8,128)}) fusion(pred[256,512]{1,0:T(8,128)(4,1)S(1)} %iota_compare_fusion.2, bf16[2,512,8,3,128]{4,1,3,2,0:T(8,128)(2,1)} %get-tuple-element.163, s32[]{:T(128)S(6)} %select_n.28, bf16[2,512,8,128]{3,1,2,0:T(8,128)(2,1)S(1)} %get-tuple-element.164), kind=kOutput, calls=%fused_computation.76.clone.1 | convolution fusion | flops 1635779072 | bytes 30588932 | tf_op jit(solution)/shard_map/while/body/eval_jaxpr/sub | solution.py:47
  295.0 12.4 %bitcast_dynamic-update-slice_fusion.2 = bf16[2,2,256,8,3,128]{5,2,4,3,1,0:T(8,128)(2,1)} fusion(bf16[2,2,256,8,3,128]{5,2,4,3,1,0:T(8,128)(2,1)} %get-tuple-element.151, s32[]{:T(128)} %get-tuple-element.150, f32[2,8,3,256,512]{4,3,2,1,0:T(8,128)} %get-tuple-element.138, f32[2,8,3,256]{3,2,1,0:T(4,128)S(1)} %get-tuple-element.139, ...), kind=kOutput, calls=%fused_computation.13.clone.1 | convolution fusion | flops 1624768512 | bytes 30458368 | tf_op jit(solution)/shard_map/while/body/eval_jaxpr/bgrqk,bkgd->bqgrd/dot_general | solution.py:48
  307.4 16.2 %copy.35 = bf16[2,2,256,8,3,128]{2,1,5,4,3,0:T(2,128)(2,1)} copy(bf16[2,2,256,8,3,128]{5,2,4,3,0,1:T(8,128)(2,1)} %bitcast.110) | data formatting | bytes 12582912 | tf_op jit(solution)/shard_map/transpose | solution.py:52
  323.6 10.8 %reshape.73 = bf16[2,512,3072]{1,2,0:T(8,128)(2,1)} reshape(bf16[2,2,256,8,3,128]{2,1,5,4,3,0:T(2,128)(2,1)} %copy.35) | data formatting | bytes 12582912 | tf_op jit(solution)/shard_map/reshape | solution.py:52
  334.4 0.0 copy-start.6
  334.4 27.5 %fusion.50 = (f32[2,512]{1,0:T(2,128)S(1)}, bf16[2,512,3072]{2,1,0:T(8,128)(2,1)}) fusion(bf16[2,512,3072]{1,2,0:T(8,128)(2,1)} %reshape.73, bf16[1,3072,3072]{2,1,0:T(8,128)(2,1)} %all-gather.21.cloned.1.call-done, bf16[2,512,3072]{2,1,0:T(8,128)(2,1)} %param.14), kind=kOutput, calls=%fused_computation.52 | convolution fusion | flops 19346227200 | bytes 37752832 | tf_op jit(solution)/shard_map/btn,nd->btd/dot_general | solution.py:66
  361.8 40.6 %all-gather.23.cloned.1.call-done = bf16[1,3072,8192]{2,1,0:T(8,128)(2,1)} async-done(((bf16[1,96,8192]{2,1,0:T(8,128)(2,1)}), bf16[1,3072,8192]{2,1,0:T(8,128)(2,1)}) %all-gather.23.cloned.1.call-update) | async-done | bytes 50331664 | tf_op jit(solution)/shard_map/all_gather | solution.py:90
  402.5 0.0 copy-done.6
  402.5 60.3 %fusion.35 = f32[2,512,8192]{2,1,0:T(8,128)} fusion(bf16[1,3072,8192]{2,1,0:T(8,128)(2,1)} %all-gather.23.cloned.1.call-done, bf16[2,512,3072]{2,1,0:T(8,128)(2,1)} %get-tuple-element.96, f32[3072]{0:T(1024)S(1)} %bitcast.116, f32[2,512]{1,0:T(2,128)S(1)} %add_rsqrt_fusion.1), kind=kOutput, calls=%fused_computation.30 | convolution fusion | flops 51552190464 | bytes 90193920 | tf_op jit(solution)/shard_map/btd,df->btf/dot_general | solution.py:69
  462.7 92.9 %all-gather.25.cloned.1.call-done = bf16[1,3072,8192]{2,1,0:T(8,128)(2,1)} async-done(((bf16[1,96,8192]{2,1,0:T(8,128)(2,1)}), bf16[1,3072,8192]{2,1,0:T(8,128)(2,1)}) %all-gather.25.cloned.1.call-update) | async-done | bytes 50331664 | tf_op jit(solution)/shard_map/all_gather | solution.py:91
  555.7 63.2 %multiply_convert_fusion = bf16[2,512,8192]{2,1,0:T(8,128)(2,1)} fusion(f32[2,512,8192]{2,1,0:T(8,128)} %fusion.35, bf16[1,3072,8192]{2,1,0:T(8,128)(2,1)} %all-gather.25.cloned.1.call-done, bf16[2,512,3072]{2,1,0:T(8,128)(2,1)} %get-tuple-element.96, f32[3072]{0:T(1024)S(1)} %bitcast.117, f32[2,512]{1,0:T(2,128)S(1)} %add_rsqrt_fusion.1), kind=kOutput, calls=%fused_computation.32 | convolution fusion | flops 51602522112 | bytes 106971136 | tf_op jit(solution)/shard_map/btd,df->btf/dot_general | solution.py:70
  618.9 90.2 %all-gather.27.cloned.1.call-done = bf16[1,8192,3072]{2,1,0:T(8,128)(2,1)} async-done(((bf16[1,256,3072]{2,1,0:T(8,128)(2,1)}), bf16[1,8192,3072]{2,1,0:T(8,128)(2,1)}) %all-gather.27.cloned.1.call-update) | async-done | bytes 50331664 | tf_op jit(solution)/shard_map/all_gather | solution.py:92
  709.1 62.3 %fusion.43 = (f32[2,512]{1,0:T(2,128)S(1)}, bf16[2,512,3072]{2,1,0:T(8,128)(2,1)S(1)}) fusion(bf16[2,512,8192]{2,1,0:T(8,128)(2,1)} %multiply_convert_fusion, bf16[1,8192,3072]{2,1,0:T(8,128)(2,1)} %all-gather.27.cloned.1.call-done, bf16[2,512,3072]{2,1,0:T(8,128)(2,1)} %get-tuple-element.96), kind=kOutput, calls=%fused_computation.45 | convolution fusion | flops 51558481920 | bytes 79695872 | tf_op jit(solution)/shard_map/btf,fd->btd/dot_general | solution.py:72
  771.4 0.0 copy-done.3
  771.4 5.5 fusion.45
  (11 shorter events, 0.1 us)
Async XLA Ops:
  6.5 6.1 copy-start.4
  6.5 51.0 %all-gather.17.cloned.1.call-start = ((), (), s32[]{:S(2)}) async-start(), calls=%async_computation.1 | async-start | bytes 6488064 | tf_op jit(solution)/shard_map/all_gather | solution.py:87
  7.3 94.9 %all-gather.19.cloned.1.call-start = ((), (), s32[]{:S(2)}) async-start(), calls=%async_computation.2 | async-start | bytes 6488064 | tf_op jit(solution)/shard_map/all_gather | solution.py:88
  9.1 166.2 %all-gather.15.cloned.1.call-start = ((), (), s32[]{:S(2)}) async-start(), calls=%async_computation | async-start | bytes 19464192 | tf_op jit(solution)/shard_map/all_gather | solution.py:86
  9.9 324.5 %all-gather.21.cloned.1.call-start = ((), (), s32[]{:S(2)}) async-start(), calls=%async_computation.3 | async-start | bytes 19464192 | tf_op jit(solution)/shard_map/all_gather | solution.py:89
  10.5 392.0 %all-gather.23.cloned.1.call-start = ((), (), s32[]{:S(2)}) async-start(), calls=%async_computation.4 | async-start | bytes 51904512 | tf_op jit(solution)/shard_map/all_gather | solution.py:90
  11.2 544.5 %all-gather.25.cloned.1.call-start = ((), (), s32[]{:S(2)}) async-start(), calls=%async_computation.5 | async-start | bytes 51904512 | tf_op jit(solution)/shard_map/all_gather | solution.py:91
  11.8 697.3 %all-gather.27.cloned.1.call-start = ((), (), s32[]{:S(2)}) async-start(), calls=%async_computation.6 | async-start | bytes 51904512 | tf_op jit(solution)/shard_map/all_gather | solution.py:92
  17.7 59.6 %copy-start = (f32[2,512,64]{1,2,0:T(8,128)}, f32[2,512,64]{1,2,0:T(8,128)S(1)}, u32[]{:S(2)}) copy-start(f32[2,512,64]{1,2,0:T(8,128)S(1)} %get-tuple-element.94) | copy-start | bytes 786436
  17.8 48.8 %copy-start.5 = (f32[1,3072]{1,0:T(1,128)S(1)}, f32[1,3072]{1,0:T(1,128)}, u32[]{:S(2)}) copy-start(f32[1,3072]{1,0:T(1,128)} %param.16) | copy-start | bytes 36868
  199.4 25.4 %copy-start.1 = (f32[2,512,64]{1,2,0:T(8,128)S(1)}, f32[2,512,64]{1,2,0:T(8,128)}, u32[]{:S(2)}) copy-start(f32[2,512,64]{1,2,0:T(8,128)} %copy-done) | copy-start | bytes 786436
  239.4 9.8 %copy-start.2 = (bf16[2,512,8,128]{3,1,2,0:T(8,128)(2,1)S(1)}, bf16[2,512,8,128]{3,1,2,0:T(8,128)(2,1)}, u32[]{:S(2)}) copy-start(bf16[2,512,8,128]{3,1,2,0:T(8,128)(2,1)} %copy.34) | copy-start | bytes 6291460
  334.4 68.1 %copy-start.6 = (f32[1,3072]{1,0:T(1,128)S(1)}, f32[1,3072]{1,0:T(1,128)}, u32[]{:S(2)}) copy-start(f32[1,3072]{1,0:T(1,128)} %param.17) | copy-start | bytes 36868
  618.8 152.6 %copy-start.3 = (f32[3072]{0:T(1024)S(1)}, f32[3072]{0:T(1024)}, u32[]{:S(2)}) copy-start(f32[3072]{0:T(1024)} %param.25) | copy-start | bytes 36868
Sparse Core Ops, SparseCore 0:
  9.4 48.0 all-gather.16
  59.6 42.5 all-gather.18
  104.3 70.9 all-gather.14
  177.2 71.6 all-gather.20
  250.8 151.5 all-gather.22
  404.4 151.2 all-gather.24
  557.8 151.2 all-gather.26
where the time goes:
time: 793 us; the launch traced here: 784 us
  waiting for transfers between devices  350 us (44%)
  matrix products  316 us (40%)
  local copies, waits for them, and re-layouts  76.5 us (10%)
  other arithmetic  25 us (3%)
  between operations  14.1 us (2%)
    all_gather x1, waiting for transfers between devices, local_forward(): full_up = lax.all_gather(w_up[layer_idx], 'wg', axis=0, tiled=True)  92.9 us
    all_gather x1, waiting for transfers between devices, local_forward(): full_down = lax.all_gather(w_down[layer_idx], 'wg', axis=0, tiled=True)  90.2 us
    dot_general x1, matrix products, decoder_layer(): jnp.einsum('btd,df->btf', normed, w_up, preferred_element_type=jnp.float32)  63.2 us
    dot_general x1, matrix products, decoder_layer(): jnp.einsum('btf,fd->btd', hidden, w_down, preferred_element_type=jnp.floa...  62.3 us
    all_gather x1, waiting for transfers between devices, local_forward(): full_query = lax.all_gather(w_query[layer_idx], 'wg', axis=0, tiled=True)  61.4 us
    dot_general x1, matrix products, decoder_layer(): jnp.einsum('btd,df->btf', normed, w_gate, preferred_element_type=jnp.floa...  60.3 us
    all_gather x1, waiting for transfers between devices, local_forward(): full_gate = lax.all_gather(w_gate[layer_idx], 'wg', axis=0, tiled=True)  40.6 us
    all_gather x1, waiting for transfers between devices, local_forward(): full_key = lax.all_gather(w_key[layer_idx], 'wg', axis=0, tiled=True)  39.8 us
  transfers between devices with their start and end apart: 7, of which 6 were waited for; matrix products, arithmetic and copies ran while one was open for 45% of the time, Pallas kernels for 0%

commit v1 on v0

v1 whole, which is shorter than its diff:
```python
import functools
import math

import jax
import jax.numpy as jnp
from jax import lax
from jax.experimental import pallas as pl
from jax.experimental.pallas import tpu as pltpu
from jax.sharding import PartitionSpec as P

EPS = 1e-5
ROPE_BASE = 10000.0
COLS_A = 512
COLS_B = 256
HALF_FF = COLS_A // 2
LAG = 5
RING = 4
N_RECV = 18
MESH = pl.DeviceIdType.MESH

R_M0, R_P0, R_2A, R_2B = 0, 1, 2, 3
R_0M, R_MM, R_PM, R_2M, R_0N, R_MN = 4, 5, 6, 7, 8, 9
R_0P, R_MP, R_PP, R_2P, R_P2, R_22 = 10, 11, 12, 13, 14, 15
R_TWIN, R_OWN = 16, 17


def rms_norm(values_in, gain_vec):
    as_f32 = values_in.astype(jnp.float32)
    mean_sq = jnp.mean(as_f32 * as_f32, axis=-1, keepdims=True)
    return (as_f32 * lax.rsqrt(mean_sq + EPS) * gain_vec).astype(jnp.bfloat16)


def rope_tables(positions, head_dim):
    half_dim = head_dim // 2
    exponents = jnp.arange(half_dim, dtype=jnp.float32) * (2.0 / head_dim)
    inv_freq = jnp.power(jnp.float32(ROPE_BASE), -exponents)
    angles = positions.astype(jnp.float32)[..., None] * inv_freq
    cos, sin = jnp.cos(angles), jnp.sin(angles)
    return jnp.concatenate([cos, cos], -1), jnp.concatenate([-sin, sin], -1)


class Place:
    def __init__(self):
        me = lax.axis_index('wg')
        self.core = lax.rem(me, 2)
        chip = me // 2
        col, row = lax.rem(chip, RING), chip // RING
        core = self.core
        self.chip = {}
        for dp in (-1, 0, 1, 2):
            for ds in (-1, 0, 1, 2):
                cc = lax.rem(col + dp * (1 - core) + ds * core + RING, RING)
                rr = lax.rem(row + dp * core + ds * (1 - core) + RING, RING)
                self.chip[dp, ds] = rr * RING + cc
        dev = lambda dp, ds: self.chip[dp, ds] * 2 + core
        self.p_up, self.p_dn = dev(1, 0), dev(-1, 0)
        self.s_up, self.s_dn = dev(0, 1), dev(0, -1)
        self.twin = chip * 2 + 1 - core
        self.me = me


class Gather:
    def __init__(self, place, local, full, recv, send, twin_send):
        self.pl, self.local, self.full = place, local, full
        self.recv, self.send_sem, self.twin_send = recv, send, twin_send
        self.half = local.shape[1] // 2

    def spot(self, blk, rel, part=None):
        ref = self.full.at[blk, self.pl.chip[rel], self.pl.core]
        if part is not None:
            ref = ref.at[pl.ds(part * self.half, self.half)]
        return ref

    def copy(self, blk, src, dst, r, dev):
        return pltpu.make_async_remote_copy(
            src_ref=src, dst_ref=dst, send_sem=self.send_sem.at[blk],
            recv_sem=self.recv.at[blk, r], device_id={'wg': dev}, device_id_type=MESH)

    def put(self, blk, rel, r, dev, part=None):
        ref = self.spot(blk, rel, part)
        self.copy(blk, ref, ref, r, dev).start()

    def got(self, blk, rel, r, part=None):
        ref = self.spot(blk, rel, part)
        self.copy(blk, ref, ref, r, self.pl.me).wait_recv()

    def own_copy(self, blk):
        return pltpu.make_async_copy(self.local.at[blk], self.spot(blk, (0, 0)), self.recv.at[blk, R_OWN])

    def twin_copy(self, blk, core):
        ref = self.full.at[blk, :, core]
        return pltpu.make_async_remote_copy(
            src_ref=ref, dst_ref=ref, send_sem=self.twin_send.at[blk],
            recv_sem=self.recv.at[blk, R_TWIN], device_id={'wg': self.pl.twin}, device_id_type=MESH)

    def stage(self, lag, blk):
        w, got, put = self.pl, self.got, self.put
        if lag == 0:
            src, dst = self.local.at[blk], self.spot(blk, (0, 0))
            self.copy(blk, src, dst, R_M0, w.p_up).start()
            self.copy(blk, src, dst, R_P0, w.p_dn).start()
            self.copy(blk, src, dst, R_0M, w.s_up).start()
            self.copy(blk, src, dst, R_0P, w.s_dn).start()
            self.own_copy(blk).start()
        elif lag == 1:
            got(blk, (-1, 0), R_M0)
            put(blk, (-1, 0), R_2A, w.p_up, 0)
            put(blk, (-1, 0), R_MM, w.s_up)
            put(blk, (-1, 0), R_MP, w.s_dn)
            got(blk, (1, 0), R_P0)
            put(blk, (1, 0), R_2B, w.p_dn, 1)
            put(blk, (1, 0), R_PM, w.s_up)
            put(blk, (1, 0), R_PP, w.s_dn)
            got(blk, (0, -1), R_0M)
            put(blk, (0, -1), R_0N, w.s_up)
        elif lag == 2:
            got(blk, (2, 0), R_2A, 0)
            got(blk, (2, 0), R_2B, 1)
            put(blk, (2, 0), R_2M, w.s_up)
            put(blk, (2, 0), R_2P, w.s_dn)
            got(blk, (-1, -1), R_MM)
            put(blk, (-1, -1), R_MN, w.s_up)
            got(blk, (1, 1), R_PP)
            put(blk, (1, 1), R_P2, w.s_dn)
        elif lag == 3:
            got(blk, (2, 1), R_2P)
            put(blk, (2, 1), R_22, w.s_dn)
        elif lag == 4:
            for rel, r in (((1, -1), R_PM), ((2, -1), R_2M), ((0, 1), R_0P), ((-1, 1), R_MP),
                           ((0, 2), R_0N), ((-1, 2), R_MN), ((1, 2), R_P2), ((2, 2), R_22)):
                got(blk, rel, r)
            self.own_copy(blk).wait()
            self.twin_copy(blk, w.core).start()
        else:
            self.twin_copy(blk, 1 - w.core).wait_recv()

    def drain(self, blk):
        whole = self.full.at[blk, pl.ds(0, RING * RING - 1), 0]
        pltpu.make_async_copy(whole, whole, self.send_sem.at[blk]).wait()
        self.twin_copy(blk, self.pl.core).wait_send()


def layer_kernel(dims, h0, w_a, w_b, cos, sin, gain_attn, gain_mlp, h_out, full_a, full_b,
                 h_s, a_s, heads, u_s, buf_a, buf_b, recv_a, recv_b, send_a, send_b, twin_a, twin_b, load_a, load_b, io_sem):
    n_seq, seq_len, n_heads, kv_heads, head_dim = dims
    n_tok, width = h_s.shape
    n_rep = n_heads // kv_heads
    per_blk = COLS_A // head_dim
    n_a, n_b = w_a.shape[0], w_b.shape[0]
    n_qk, n_v = (n_heads + kv_heads) // per_blk, kv_heads // per_blk
    n_wo = width // COLS_A
    n_gu = u_s.shape[1] // HALF_FF
    first_gu = n_qk + n_v + n_wo
    place = Place()
    ga = Gather(place, w_a, full_a, recv_a, send_a, twin_a)
    gb = Gather(place, w_b, full_b, recv_b, send_b, twin_b)

    barrier = pltpu.get_barrier_semaphore()
    near = (place.p_up, place.p_dn, place.s_up, place.s_dn, place.twin)
    for dev in near:
        pl.semaphore_signal(barrier, inc=1, device_id={'wg': dev}, device_id_type=MESH)
    pl.semaphore_wait(barrier, len(near))

    def tick(t, may_a=True, may_b=True):
        for lag in range(LAG + 1):
            blk = t - lag
            if may_a:
                @pl.when(jnp.logical_and(blk >= 0, blk < n_a))
                def _():
                    ga.stage(lag, blk)
            if may_b:
                @pl.when(jnp.logical_and(blk >= n_a, blk < n_a + n_b))
                def _():
                    gb.stage(lag, blk - n_a)

    def load_copy_a(i):
        slot = lax.rem(i, 2)
        return pltpu.make_async_copy(full_a.at[i], buf_a.at[slot], load_a.at[slot])

    def load_copy_b(i):
        slot = lax.rem(i, 2)
        return pltpu.make_async_copy(full_b.at[i], buf_b.at[slot], load_b.at[slot])

    def weights_a(i):
        return buf_a[lax.rem(i, 2)].reshape(-1, COLS_A)

    def weights_b(i):
        return buf_b[lax.rem(i, 2)].reshape(-1, COLS_B)

    def dot(x, w):
        return jnp.dot(x, w, preferred_element_type=jnp.float32)

    def norm_into(gain):
        rows = min(64, seq_len)

        def body(i, _):
            sl = pl.ds(pl.multiple_of(i * rows, rows), rows)
            a_s[sl, :] = rms_norm(h_s[sl, :], gain[...])
            return 0
        lax.fori_loop(0, n_tok // rows, body, 0)

    def over_seqs(body):
        def step(b, _):
            body(pl.ds(pl.multiple_of(b * seq_len, seq_len), seq_len))
            return 0
        lax.fori_loop(0, n_seq, step, 0)

    def project(i, rope):
        load_copy_a(i).wait()
        load_copy_a(i + 1).start()

        def body(rows):
            out = dot(a_s[rows, :], weights_a(i)).astype(jnp.bfloat16)
            for j in range(per_blk):
                one = out[:, j * head_dim:(j + 1) * head_dim]
                if rope:
                    one = one.astype(jnp.float32)
                    one = (one * cos[rows, :] + pltpu.roll(one, head_dim // 2, 1) * sin[rows, :]).astype(jnp.bfloat16)
                heads[i * per_blk + j, rows, :] = one
        over_seqs(body)

    q_block = seq_len // 2

    def attend(n):
        seq, group = n // kv_heads, lax.rem(n, kv_heads)
        start = pl.multiple_of(seq * seq_len, seq_len)
        for qb in range(2):
            n_keys = (qb + 1) * q_block
            keys = heads[n_heads + group, pl.ds(start, n_keys), :]
            vals = heads[n_heads + kv_heads + group, pl.ds(start, n_keys), :]
            q_rows = pl.ds(pl.multiple_of(start + qb * q_block, q_block), q_block)
            q_idx = qb * q_block + lax.broadcasted_iota(jnp.int32, (q_block, n_keys), 0)
            k_idx = lax.broadcasted_iota(jnp.int32, (q_block, n_keys), 1)
            for r in range(n_rep):
                head = group * n_rep + r
                scores = lax.dot_general(heads[head, q_rows, :], keys, (((1,), (1,)), ((), ())),
                                         preferred_element_type=jnp.float32) * head_dim ** -0.5
                scores = jnp.where(k_idx <= q_idx, scores, -1e30)
                top = jnp.max(scores, axis=-1, keepdims=True)
                expd = jnp.exp(scores - top)
                total = jnp.sum(expd, axis=-1, keepdims=True)
                probs = (expd / total).astype(jnp.bfloat16)
                cols = pl.ds(pl.multiple_of(head * head_dim, head_dim), head_dim)
                a_s[q_rows, cols] = dot(probs, vals).astype(jnp.bfloat16)

    def project_out(i):
        blk = n_qk + n_v + i
        load_copy_a(blk).wait()
        load_copy_a(blk + 1).start()
        cols = pl.ds(pl.multiple_of(i * COLS_A, COLS_A), COLS_A)

        def body(rows):
            out = dot(a_s[rows, :], weights_a(blk))
            h_s[rows, cols] = (h_s[rows, cols].astype(jnp.float32) + out).astype(jnp.bfloat16)
        over_seqs(body)

    def gate_up(i):
        blk = first_gu + i
        load_copy_a(blk).wait()

        @pl.when(i + 1 < n_gu)
        def _():
            load_copy_a(blk + 1).start()

        @pl.when(i + 1 == n_gu)
        def _():
            load_copy_b(0).start()
        cols = pl.ds(pl.multiple_of(i * HALF_FF, HALF_FF), HALF_FF)

        def body(rows):
            out = dot(a_s[rows, :], weights_a(blk))
            gate, up = out[:, :HALF_FF], out[:, HALF_FF:]
            u_s[rows, cols] = (gate * jax.nn.sigmoid(gate) * up).astype(jnp.bfloat16)
        over_seqs(body)

    def down(i):
        load_copy_b(i).wait()

        @pl.when(i + 1 < n_b)
        def _():
            load_copy_b(i + 1).start()
        cols = pl.ds(pl.multiple_of(i * COLS_B, COLS_B), COLS_B)

        def body(rows):
            out = dot(u_s[rows, :], weights_b(i))
            h_s[rows, cols] = (h_s[rows, cols].astype(jnp.float32) + out).astype(jnp.bfloat16)
        over_seqs(body)

    def loop(lo, hi, body):
        def step(i, _):
            body(i)
            return 0
        lax.fori_loop(lo, hi, step, 0)

    h_in = pltpu.make_async_copy(h0, h_s, io_sem.at[0])
    h_in.start()
    tick(0, may_b=False)
    h_in.wait()
    norm_into(gain_attn)
    now = 1
    only_a = functools.partial(tick, may_b=n_a <= 0)
    assert n_a > LAG + 1 + n_qk + n_v + n_seq * kv_heads // 2 + n_wo
    loop(now, LAG + 1, only_a)
    now = LAG + 1
    load_copy_a(0).start()

    def seg_qk(i):
        only_a(i + LAG + 1)
        project(i, True)

    def seg_v(i):
        only_a(i + LAG + 1)
        project(i, False)
    loop(0, n_qk, seg_qk)
    loop(n_qk, n_qk + n_v, seg_v)
    now += n_qk + n_v
    att_from = now

    def seg_att(i):
        only_a(att_from + i)
        attend(2 * i)
        attend(2 * i + 1)
    n_att = n_seq * kv_heads // 2
    loop(0, n_att, seg_att)
    now += n_att
    wo_from = now

    def seg_wo(i):
        only_a(wo_from + i)
        project_out(i)
    loop(0, n_wo, seg_wo)
    now += n_wo
    norm_into(gain_mlp)
    rounds = n_gu // 4
    need = max(first_gu + 4 * i + 4 + LAG - (3 * i + 2) for i in range(rounds))
    if now < need:
        loop(now, need, tick)
        now = need
    gu_from = now

    def seg_gu(i):
        t = gu_from + 3 * i
        tick(t)
        gate_up(4 * i)
        tick(t + 1)
        gate_up(4 * i + 1)
        tick(t + 2)
        gate_up(4 * i + 2)
        gate_up(4 * i + 3)
    loop(0, rounds, seg_gu)
    now += 3 * rounds
    need = n_a + LAG + 1
    if now < need:
        loop(now, need, tick)
        now = need
    down_from = now
    late = functools.partial(tick, may_a=down_from < n_a + LAG)

    def seg_down(i):
        late(down_from + i)
        down(i)
    loop(0, n_b, seg_down)

    out_copy = pltpu.make_async_copy(h_s, h_out, io_sem.at[1])
    out_copy.start()
    loop(0, n_a, ga.drain)
    loop(0, n_b, gb.drain)
    out_copy.wait()


def run_layer(h0, cos, sin, gain_attn, gain_mlp, w_query, w_key, w_value, w_out, w_gate, w_up, w_down, n_dev):
    n_seq, seq_len, width = h0.shape
    rows, n_heads, head_dim = w_query.shape
    kv_heads = w_key.shape[1]
    n_tok = n_seq * seq_len
    ff = w_gate.shape[1]
    rows_b = w_down.shape[0]

    def blocks(weight, cols):
        return weight.reshape(weight.shape[0], -1, cols).transpose(1, 0, 2)

    gu = jnp.concatenate([blocks(w_gate, HALF_FF), blocks(w_up, HALF_FF)], axis=-1)
    w_a = jnp.concatenate([
        blocks(w_query.reshape(rows, -1), COLS_A), blocks(w_key.reshape(rows, -1), COLS_A),
        blocks(w_value.reshape(rows, -1), COLS_A), blocks(w_out, COLS_A), gu], axis=0)
    w_b = blocks(w_down, COLS_B)
    n_a, n_b = w_a.shape[0], w_b.shape[0]
    chips = n_dev // 2
    any_spec = pl.BlockSpec(memory_space=pl.ANY)
    vmem_spec = pl.BlockSpec(memory_space=pltpu.VMEM)
    flops = 2 * n_tok * n_dev * (w_a.size + w_b.size)
    h_out, _, _ = pl.pallas_call(
        functools.partial(layer_kernel, (n_seq, seq_len, n_heads, kv_heads, head_dim)),
        out_shape=(
            jax.ShapeDtypeStruct((n_tok, width), jnp.bfloat16),
            jax.ShapeDtypeStruct((n_a, chips, 2, rows, COLS_A), jnp.bfloat16),
            jax.ShapeDtypeStruct((n_b, chips, 2, rows_b, COLS_B), jnp.bfloat16),
        ),
        in_specs=[any_spec] * 3 + [vmem_spec] * 4,
        out_specs=(any_spec,) * 3,
        scratch_shapes=[
            pltpu.VMEM((n_tok, width), jnp.bfloat16),
            pltpu.VMEM((n_tok, width), jnp.bfloat16),
            pltpu.VMEM((n_heads + 2 * kv_heads, n_tok, head_dim), jnp.bfloat16),
            pltpu.VMEM((n_tok, ff), jnp.bfloat16),
            pltpu.VMEM((2, chips, 2, rows, COLS_A), jnp.bfloat16),
            pltpu.VMEM((2, chips, 2, rows_b, COLS_B), jnp.bfloat16),
            pltpu.SemaphoreType.DMA((n_a, N_RECV)),
            pltpu.SemaphoreType.DMA((n_b, N_RECV)),
            pltpu.SemaphoreType.DMA((n_a,)),
            pltpu.SemaphoreType.DMA((n_b,)),
            pltpu.SemaphoreType.DMA((n_a,)),
            pltpu.SemaphoreType.DMA((n_b,)),
            pltpu.SemaphoreType.DMA((2,)),
            pltpu.SemaphoreType.DMA((2,)),
            pltpu.SemaphoreType.DMA((2,)),
        ],
        compiler_params=pltpu.CompilerParams(
            collective_id=0, has_side_effects=True, vmem_limit_bytes=66_000_000),
        cost_estimate=pl.CostEstimate(flops=flops, bytes_accessed=4 * n_dev * (w_a.size + w_b.size), transcendentals=0),
        name='prefill_layer',
    )(h0.reshape(n_tok, width), w_a, w_b, cos, sin, gain_attn[None], gain_mlp[None])
    return h_out.reshape(n_seq, seq_len, width)


def solution(mesh):
    token_spec = P(('data', 'wg'))
    weight_spec = P(None, 'wg')
    whole_spec = P()
    in_specs = (token_spec, token_spec, whole_spec, whole_spec, weight_spec, weight_spec, weight_spec, weight_spec, weight_spec, weight_spec, weight_spec, whole_spec)
    n_dev = mesh.shape['wg']
    assert n_dev == 2 * RING * RING

    def local_forward(h0, positions, norm_attn, norm_mlp, w_query, w_key, w_value, w_out, w_gate, w_up, w_down, norm_final):
        cos, sin = rope_tables(positions.reshape(-1), w_query.shape[-1])
        residual = h0
        for l in range(w_query.shape[0]):
            residual = run_layer(residual, cos, sin, norm_attn[l], norm_mlp[l], w_query[l], w_key[l], w_value[l],
                                 w_out[l], w_gate[l], w_up[l], w_down[l], n_dev)
        return rms_norm(residual, norm_final)

    return jax.shard_map(local_forward, mesh=mesh, in_specs=in_specs, out_specs=token_spec, check_vma=False)
```

time: 793 us -> 607 us (0.77); the launches traced: 784 us -> 607 us
  Pallas kernels: 0 us -> 567 us
  waiting for transfers between devices: 350 us -> 0 us
  matrix products: 316 us -> 0 us
  local copies, waits for them, and re-layouts: 76.5 us -> 19.6 us
  between operations: 14.1 us -> 0.09 us
    pallas_call x0 -> x1, Pallas kernels: none -> 567 us  [run_layer(): pl.pallas_call(functools.partial(layer_kernel, (n_seq, seq_len, n_heads,...]
    all_gather x7 -> x0, waiting for transfers between devices: 346 us -> none  [the longest x1 92.9 us: local_forward(): full_up = lax.all_gather(w_up[layer_idx], 'wg', axis=0, tiled=True)]
    dot_general x9 -> x0, matrix products: 286 us -> none  [the longest x1 63.2 us: decoder_layer(): jnp.einsum('btd,df->btf', normed, w_up, preferred_element_type=jnp.float32)]
    all_gather x2 -> x0, local copies, waits for them, and re-layouts: 33.1 us -> none  [the longest x1 24.1 us: local_forward(): full_query = lax.all_gather(w_query[layer_idx], 'wg', axis=0, tiled=True)]
    sub x2 -> x0, matrix products: 30.5 us -> none  [one_block(): attn_probs = jax.nn.softmax(scores, axis=-1).astype(jnp.bfloat16)]
    transpose x1, local copies, waits for them, and re-layouts: 16.2 us -> 2.97 us  [blocks(): return weight.reshape(weight.shape[0], -1, cols).transpose(1, 0, 2)]
    concatenate x2 -> x0, local copies, waits for them, and re-layouts: 11.1 us -> none  [apply_rope(): jnp.concatenate([first_half * cos_table - second_half * sin_table, second...]
    reshape x1 -> x0, local copies, waits for them, and re-layouts: 10.8 us -> none  [causal_attention(): jnp.moveaxis(attended, 0, 1)]
  transfers between devices with their start and end apart: 7 -> 0, of which waited for: 6 -> 0; matrix products, arithmetic and copies ran while one was open for 45% -> 0% of each run, Pallas kernels for 0% -> 0%
where the time goes in v1:
time: 607 us
  Pallas kernels  567 us (93%)
  local copies, waits for them, and re-layouts  19.6 us (3%)
  other arithmetic  19.5 us (3%)
    pallas_call x1, Pallas kernels, run_layer(): pl.pallas_call(functools.partial(layer_kernel, (n_seq, seq_len, n_heads,...  567 us

profile of v1, /device:TPU:97, one launch (start us, length us, event | category | flops | bytes accessed | tf_op | source)
XLA Modules:
  0.0 606.6 jit_solution(240635326467377254)
XLA Ops:
  0.0 0.0 copy-start
  0.0 0.8 convert_bitcast_fusion
  0.8 1.0 reshape_reshape_squeeze.10
  1.8 1.0 reshape_reshape_squeeze.11
  2.8 0.0 copy-start.1
  2.9 2.3 reshape_reshape_squeeze.9
  5.2 2.5 reshape_squeeze.12
  7.7 1.9 fusion
  9.6 1.4 pad_maximum_fusion
  11.0 0.0 copy-done
  11.0 0.4 copy.21
  11.4 0.0 copy-done.1
  11.4 0.4 copy.22
  11.9 3.0 copy_bitcast_fusion
  14.8 1.7 copy.19
  16.5 1.6 copy.20
  18.1 2.1 bitcast_dynamic-update-slice_fusion.1
  20.2 0.7 bitcast_dynamic-update-slice_fusion.3
  20.9 0.7 bitcast_dynamic-update-slice_fusion.2
  21.6 2.1 bitcast_dynamic-update-slice_fusion
  23.8 3.3 maximum_dynamic-update-slice_fusion.w_a
  27.1 567.3 %prefill_layer.1 = (bf16[1024,3072]{1,0:T(8,128)(2,1)}, bf16[48,16,2,96,512]{4,3,2,1,0:T(8,128)(2,1)}, bf16[12,16,2,256,256]{4,3,2,1,0:T(8,128)(2,1)}) custom-call(bf16[1024,3072]{1,0:T(8,128)(2,1)} %bitcast.40, bf16[48,96,512]{2,1,0:T(8,128)(2,1)} %maximum_dynamic-update-slice_fusion.w_a, bf16[12,256,256]{2,1,0:T(8,128)(2,1)} %bitcast.38, ...), custom_call_target="tpu_custom_call" | custom-call | flops 206158430208 | bytes 402653184 | tf_op jit(solution)/shard_map/prefill_layer/pallas_call | solution.py:392
  594.4 0.0 copy-start.2
  594.4 4.1 multiply_reduce_fusion
  598.6 0.0 copy-done.2
  598.6 8.0 %multiply_convert_fusion = bf16[2,512,3072]{2,1,0:T(8,128)(2,1)} fusion(f32[3072]{0:T(1024)S(1)} %copy-done.2, f32[2,512]{1,0:T(2,128)S(1)} %rsqrt.12, bf16[2,512,3072]{2,1,0:T(8,128)(2,1)} %bitcast.32), kind=kLoop, calls=%fused_computation | loop fusion | flops 12582912 | bytes 12599296 | tf_op jit(solution)/shard_map/convert_element_type | solution.py:30
  (4 shorter events, 0.0 us)
Async XLA Ops:
  0.0 11.0 %copy-start = (bf16[1,96,8192]{2,1,0:T(8,128)(2,1)S(1)}, bf16[1,96,8192]{2,1,0:T(8,128)(2,1)}, u32[]{:S(2)}) copy-start(bf16[1,96,8192]{2,1,0:T(8,128)(2,1)} %param.20) | copy-start | bytes 4718596
  2.8 8.6 %copy-start.1 = (bf16[1,96,8192]{2,1,0:T(8,128)(2,1)S(1)}, bf16[1,96,8192]{2,1,0:T(8,128)(2,1)}, u32[]{:S(2)}) copy-start(bf16[1,96,8192]{2,1,0:T(8,128)(2,1)} %param.21) | copy-start | bytes 4718596
  594.4 4.1 copy-start.2

commit v2 on v1

--- a/solution.py
+++ b/solution.py
@@ -10,9 +10,7 @@
 
 EPS = 1e-5
 ROPE_BASE = 10000.0
-COLS_A = 512
-COLS_B = 256
-HALF_FF = COLS_A // 2
+COLS = 256
 LAG = 5
 RING = 4
 N_RECV = 18
@@ -32,11 +30,11 @@
 
 def rope_tables(positions, head_dim):
     half_dim = head_dim // 2
-    exponents = jnp.arange(half_dim, dtype=jnp.float32) * (2.0 / head_dim)
+    lane = jnp.arange(head_dim)
+    exponents = (lane % half_dim).astype(jnp.float32) * (2.0 / head_dim)
     inv_freq = jnp.power(jnp.float32(ROPE_BASE), -exponents)
     angles = positions.astype(jnp.float32)[..., None] * inv_freq
-    cos, sin = jnp.cos(angles), jnp.sin(angles)
-    return jnp.concatenate([cos, cos], -1), jnp.concatenate([-sin, sin], -1)
+    return jnp.cos(angles), jnp.where(lane < half_dim, -1.0, 1.0) * jnp.sin(angles)
 
 
 class Place:
@@ -60,16 +58,13 @@
 
 
 class Gather:
-    def __init__(self, place, local, full, recv, send, twin_send):
-        self.pl, self.local, self.full = place, local, full
+    def __init__(self, place, own, full, recv, send, twin_send):
+        self.pl, self.own, self.full = place, own, full
         self.recv, self.send_sem, self.twin_send = recv, send, twin_send
-        self.half = local.shape[1] // 2
 
     def spot(self, blk, rel, part=None):
         ref = self.full.at[blk, self.pl.chip[rel], self.pl.core]
-        if part is not None:
-            ref = ref.at[pl.ds(part * self.half, self.half)]
-        return ref
+        return ref if part is None else ref.at[part]
 
     def copy(self, blk, src, dst, r, dev):
         return pltpu.make_async_remote_copy(
@@ -84,8 +79,17 @@
         ref = self.spot(blk, rel, part)
         self.copy(blk, ref, ref, r, self.pl.me).wait_recv()
 
-    def own_copy(self, blk):
-        return pltpu.make_async_copy(self.local.at[blk], self.spot(blk, (0, 0)), self.recv.at[blk, R_OWN])
+    def first(self, blk, own):
+        w = self.pl
+        for r, dev in ((R_M0, w.p_up), (R_P0, w.p_dn), (R_0M, w.s_up), (R_0P, w.s_dn)):
+            for part in range(2):
+                self.copy(blk, own(blk, part), self.spot(blk, (0, 0), part), r, dev).start()
+        for part in range(2):
+            pltpu.make_async_copy(own(blk, part), self.spot(blk, (0, 0), part), self.recv.at[blk, R_OWN]).start()
+
+    def own_wait(self, blk):
+        ref = self.spot(blk, (0, 0))
+        pltpu.make_async_copy(ref, ref, self.recv.at[blk, R_OWN]).wait()
 
     def twin_copy(self, blk, core):
         ref = self.full.at[blk, :, core]
@@ -96,12 +100,15 @@
     def stage(self, lag, blk):
         w, got, put = self.pl, self.got, self.put
         if lag == 0:
-            src, dst = self.local.at[blk], self.spot(blk, (0, 0))
-            self.copy(blk, src, dst, R_M0, w.p_up).start()
-            self.copy(blk, src, dst, R_P0, w.p_dn).start()
-            self.copy(blk, src, dst, R_0M, w.s_up).start()
-            self.copy(blk, src, dst, R_0P, w.s_dn).start()
-            self.own_copy(blk).start()
+            for lo, hi, own in self.own:
+                if lo == hi:
+                    continue
+                if len(self.own) == 1:
+                    self.first(blk, own)
+                else:
+                    @pl.when(jnp.logical_and(blk >= lo, blk < hi))
+                    def _():
+                        self.first(blk, own)
         elif lag == 1:
             got(blk, (-1, 0), R_M0)
             put(blk, (-1, 0), R_2A, w.p_up, 0)
@@ -129,7 +136,7 @@
             for rel, r in (((1, -1), R_PM), ((2, -1), R_2M), ((0, 1), R_0P), ((-1, 1), R_MP),
                            ((0, 2), R_0N), ((-1, 2), R_MN), ((1, 2), R_P2), ((2, 2), R_22)):
                 got(blk, rel, r)
-            self.own_copy(blk).wait()
+            self.own_wait(blk)
             self.twin_copy(blk, w.core).start()
         else:
             self.twin_copy(blk, 1 - w.core).wait_recv()
@@ -140,20 +147,41 @@
         self.twin_copy(blk, self.pl.core).wait_send()
 
 
-def layer_kernel(dims, h0, w_a, w_b, cos, sin, gain_attn, gain_mlp, h_out, full_a, full_b,
-                 h_s, a_s, heads, u_s, buf_a, buf_b, recv_a, recv_b, send_a, send_b, twin_a, twin_b, load_a, load_b, io_sem):
+def layer_kernel(dims, h0, w_q, w_k, w_v, w_o, w_g, w_u, w_d, cos, sin, gain_attn, gain_mlp, gain_out, out_ref, full_a, full_b,
+                 h_s, a_s, heads, u_s, acc_s, buf_a, buf_b, recv_a, recv_b, send_a, send_b, twin_a, twin_b, load_a, load_b, io_sem):
     n_seq, seq_len, n_heads, kv_heads, head_dim = dims
     n_tok, width = h_s.shape
     n_rep = n_heads // kv_heads
-    per_blk = COLS_A // head_dim
-    n_a, n_b = w_a.shape[0], w_b.shape[0]
-    n_qk, n_v = (n_heads + kv_heads) // per_blk, kv_heads // per_blk
-    n_wo = width // COLS_A
-    n_gu = u_s.shape[1] // HALF_FF
+    blk_cols = 2 * COLS
+    per_part = COLS // head_dim
+    n_q, n_k = n_heads * head_dim // blk_cols, kv_heads * head_dim // blk_cols
+    n_qk, n_v = n_q + n_k, n_k
+    n_wo = width // blk_cols
+    n_gu = w_g.shape[1] // COLS
     first_gu = n_qk + n_v + n_wo
+    n_a = first_gu + n_gu
+    rows_b = w_d.shape[0]
+    half_b = rows_b // 2
+    n_b = 2 * (width // COLS)
     place = Place()
-    ga = Gather(place, w_a, full_a, recv_a, send_a, twin_a)
-    gb = Gather(place, w_b, full_b, recv_b, send_b, twin_b)
+
+    def cols_of(ref, blk, part):
+        return ref.at[:, pl.ds(pl.multiple_of((2 * blk + part) * COLS, COLS), COLS)]
+
+    def ff_cols(blk, part):
+        return (w_g, w_u)[part].at[:, pl.ds(pl.multiple_of((blk - first_gu) * COLS, COLS), COLS)]
+
+    def down_part(blk, part):
+        quarter = half_b // 2
+        return w_d.at[pl.ds(pl.multiple_of(lax.rem(blk, 2) * half_b + part * quarter, quarter), quarter),
+                      pl.ds(pl.multiple_of(blk // 2 * COLS, COLS), COLS)]
+    own_a = [(0, n_q, lambda blk, part: cols_of(w_q, blk, part)),
+             (n_q, n_qk, lambda blk, part: cols_of(w_k, blk - n_q, part)),
+             (n_qk, n_qk + n_v, lambda blk, part: cols_of(w_v, blk - n_qk, part)),
+             (n_qk + n_v, first_gu, lambda blk, part: cols_of(w_o, blk - n_qk - n_v, part)),
+             (first_gu, n_a, ff_cols)]
+    ga = Gather(place, own_a, full_a, recv_a, send_a, twin_a)
+    gb = Gather(place, [(0, n_b, down_part)], full_b, recv_b, send_b, twin_b)
 
     barrier = pltpu.get_barrier_semaphore()
     near = (place.p_up, place.p_dn, place.s_up, place.s_dn, place.twin)
@@ -181,23 +209,23 @@
         slot = lax.rem(i, 2)
         return pltpu.make_async_copy(full_b.at[i], buf_b.at[slot], load_b.at[slot])
 
-    def weights_a(i):
-        return buf_a[lax.rem(i, 2)].reshape(-1, COLS_A)
+    def weights_a(i, part):
+        return buf_a[lax.rem(i, 2), :, :, part].reshape(width, COLS)
 
     def weights_b(i):
-        return buf_b[lax.rem(i, 2)].reshape(-1, COLS_B)
+        return buf_b[lax.rem(i, 2)].reshape(-1, COLS)
 
     def dot(x, w):
         return jnp.dot(x, w, preferred_element_type=jnp.float32)
 
-    def norm_into(gain):
-        rows = min(64, seq_len)
-
+    norm_rows = min(64, seq_len)
+
+    def norm_into(gain, lo, hi):
         def body(i, _):
-            sl = pl.ds(pl.multiple_of(i * rows, rows), rows)
+            sl = pl.ds(pl.multiple_of(i * norm_rows, norm_rows), norm_rows)
             a_s[sl, :] = rms_norm(h_s[sl, :], gain[...])
             return 0
-        lax.fori_loop(0, n_tok // rows, body, 0)
+        lax.fori_loop(lo, hi, body, 0)
 
     def over_seqs(body):
         def step(b, _):
@@ -210,13 +238,14 @@
         load_copy_a(i + 1).start()
 
         def body(rows):
-            out = dot(a_s[rows, :], weights_a(i)).astype(jnp.bfloat16)
-            for j in range(per_blk):
-                one = out[:, j * head_dim:(j + 1) * head_dim]
-                if rope:
-                    one = one.astype(jnp.float32)
-                    one = (one * cos[rows, :] + pltpu.roll(one, head_dim // 2, 1) * sin[rows, :]).astype(jnp.bfloat16)
-                heads[i * per_blk + j, rows, :] = one
+            for part in range(2):
+                out = dot(a_s[rows, :], weights_a(i, part)).astype(jnp.bfloat16)
+                for j in range(per_part):
+                    one = out[:, j * head_dim:(j + 1) * head_dim]
+                    if rope:
+                        one = one.astype(jnp.float32)
+                        one = (one * cos[rows, :] + pltpu.roll(one, head_dim // 2, 1) * sin[rows, :]).astype(jnp.bfloat16)
+                    heads[(2 * i + part) * per_part + j, rows, :] = one
         over_seqs(body)
 
     q_block = seq_len // 2
@@ -247,11 +276,12 @@
         blk = n_qk + n_v + i
         load_copy_a(blk).wait()
         load_copy_a(blk + 1).start()
-        cols = pl.ds(pl.multiple_of(i * COLS_A, COLS_A), COLS_A)
 
         def body(rows):
-            out = dot(a_s[rows, :], weights_a(blk))
-            h_s[rows, cols] = (h_s[rows, cols].astype(jnp.float32) + out).astype(jnp.bfloat16)
+            for part in range(2):
+                cols = pl.ds(pl.multiple_of((2 * i + part) * COLS, COLS), COLS)
+                out = dot(a_s[rows, :], weights_a(blk, part))
+                h_s[rows, cols] = (h_s[rows, cols].astype(jnp.float32) + out).astype(jnp.bfloat16)
         over_seqs(body)
 
     def gate_up(i):
@@ -265,12 +295,16 @@
         @pl.when(i + 1 == n_gu)
         def _():
             load_copy_b(0).start()
-        cols = pl.ds(pl.multiple_of(i * HALF_FF, HALF_FF), HALF_FF)
+        n_own = COLS // rows_b
 
         def body(rows):
-            out = dot(a_s[rows, :], weights_a(blk))
-            gate, up = out[:, :HALF_FF], out[:, HALF_FF:]
-            u_s[rows, cols] = (gate * jax.nn.sigmoid(gate) * up).astype(jnp.bfloat16)
+            gate = dot(a_s[rows, :], weights_a(blk, 0))
+            up = dot(a_s[rows, :], weights_a(blk, 1))
+            u = (gate * jax.nn.sigmoid(gate) * up).astype(jnp.bfloat16)
+            for j in range(n_own):
+                to = pl.ds(pl.multiple_of((i * n_own + j) * half_b, half_b), half_b)
+                for half in range(2):
+                    u_s[half, rows, to] = u[:, j * rows_b + half * half_b:j * rows_b + (half + 1) * half_b]
         over_seqs(body)
 
     def down(i):
@@ -279,12 +313,22 @@
         @pl.when(i + 1 < n_b)
         def _():
             load_copy_b(i + 1).start()
-        cols = pl.ds(pl.multiple_of(i * COLS_B, COLS_B), COLS_B)
-
-        def body(rows):
-            out = dot(u_s[rows, :], weights_b(i))
+        cols = pl.ds(pl.multiple_of(i // 2 * COLS, COLS), COLS)
+
+        def first_half(rows):
+            acc_s[rows, :] = dot(u_s[0, rows, :], weights_b(i))
+
+        def second_half(rows):
+            out = acc_s[rows, :] + dot(u_s[1, rows, :], weights_b(i))
             h_s[rows, cols] = (h_s[rows, cols].astype(jnp.float32) + out).astype(jnp.bfloat16)
-        over_seqs(body)
+
+        @pl.when(lax.rem(i, 2) == 0)
+        def _():
+            over_seqs(first_half)
+
+        @pl.when(lax.rem(i, 2) == 1)
+        def _():
+            over_seqs(second_half)
 
     def loop(lo, hi, body):
         def step(i, _):
@@ -294,13 +338,19 @@
 
     h_in = pltpu.make_async_copy(h0, h_s, io_sem.at[0])
     h_in.start()
-    tick(0, may_b=False)
+    only_a = functools.partial(tick, may_b=False)
+    n_norm = n_tok // norm_rows
+    only_a(0)
+    only_a(1)
     h_in.wait()
-    norm_into(gain_attn)
-    now = 1
-    only_a = functools.partial(tick, may_b=n_a <= 0)
+    now = 2
+    share = -(-n_norm // (LAG + 1 - now))
+
+    def seg_start(i):
+        only_a(i)
+        norm_into(gain_attn, (i - 2) * share, jnp.minimum((i - 1) * share, n_norm))
     assert n_a > LAG + 1 + n_qk + n_v + n_seq * kv_heads // 2 + n_wo
-    loop(now, LAG + 1, only_a)
+    loop(now, LAG + 1, seg_start)
     now = LAG + 1
     load_copy_a(0).start()
 
@@ -330,7 +380,7 @@
         project_out(i)
     loop(0, n_wo, seg_wo)
     now += n_wo
-    norm_into(gain_mlp)
+    norm_into(gain_mlp, 0, n_norm)
     rounds = n_gu // 4
     need = max(first_gu + 4 * i + 4 + LAG - (3 * i + 2) for i in range(rounds))
     if now < need:
@@ -361,50 +411,70 @@
         down(i)
     loop(0, n_b, seg_down)
 
-    out_copy = pltpu.make_async_copy(h_s, h_out, io_sem.at[1])
-    out_copy.start()
+    if gain_out is None:
+        out_copy = pltpu.make_async_copy(h_s, out_ref, io_sem.at[1])
+        out_copy.start()
+    else:
+        def finish(i):
+            sl = pl.ds(pl.multiple_of(i * norm_rows, norm_rows), norm_rows)
+            a_s[sl, :] = rms_norm(h_s[sl, :], gain_out[...])
+
+            @pl.when(i > 0)
+            def _():
+                put_out(i - 1)
+
+        def put_out(i):
+            sl = pl.ds(pl.multiple_of(i * norm_rows, norm_rows), norm_rows)
+            pltpu.make_async_copy(a_s.at[sl], out_ref.at[sl], io_sem.at[1]).start()
+        loop(0, n_norm, finish)
+        out_copy = pltpu.make_async_copy(a_s, out_ref, io_sem.at[1])
     loop(0, n_a, ga.drain)
     loop(0, n_b, gb.drain)
+    if gain_out is not None:
+        put_out(n_norm - 1)
     out_copy.wait()
 
 
-def run_layer(h0, cos, sin, gain_attn, gain_mlp, w_query, w_key, w_value, w_out, w_gate, w_up, w_down, n_dev):
+def run_layer(h0, cos, sin, gain_attn, gain_mlp, gain_out, w_query, w_key, w_value, w_out, w_gate, w_up, w_down, n_dev):
     n_seq, seq_len, width = h0.shape
     rows, n_heads, head_dim = w_query.shape
     kv_heads = w_key.shape[1]
     n_tok = n_seq * seq_len
     ff = w_gate.shape[1]
     rows_b = w_down.shape[0]
-
-    def blocks(weight, cols):
-        return weight.reshape(weight.shape[0], -1, cols).transpose(1, 0, 2)
-
-    gu = jnp.concatenate([blocks(w_gate, HALF_FF), blocks(w_up, HALF_FF)], axis=-1)
-    w_a = jnp.concatenate([
-        blocks(w_query.reshape(rows, -1), COLS_A), blocks(w_key.reshape(rows, -1), COLS_A),
-        blocks(w_value.reshape(rows, -1), COLS_A), blocks(w_out, COLS_A), gu], axis=0)
-    w_b = blocks(w_down, COLS_B)
-    n_a, n_b = w_a.shape[0], w_b.shape[0]
+    w_q, w_k, w_v = (w.reshape(rows, -1) for w in (w_query, w_key, w_value))
+    n_a = (w_q.shape[1] + w_k.shape[1] + w_v.shape[1] + width) // (2 * COLS) + ff // COLS
+    n_b = 2 * (width // COLS)
     chips = n_dev // 2
     any_spec = pl.BlockSpec(memory_space=pl.ANY)
     vmem_spec = pl.BlockSpec(memory_space=pltpu.VMEM)
-    flops = 2 * n_tok * n_dev * (w_a.size + w_b.size)
-    h_out, _, _ = pl.pallas_call(
-        functools.partial(layer_kernel, (n_seq, seq_len, n_heads, kv_heads, head_dim)),
+    n_weights = n_dev * (n_a * rows * 2 * COLS + rows_b * width)
+    last = gain_out is not None
+    body = functools.partial(layer_kernel, (n_seq, seq_len, n_heads, kv_heads, head_dim))
+    operands = [h0.reshape(n_tok, width), w_q, w_k, w_v, w_out, w_gate, w_up, w_down, cos, sin, gain_attn[None], gain_mlp[None]]
+    if last:
+        operands.append(gain_out[None])
+        kernel = body
+    else:
+        def kernel(*refs):
+            return body(*refs[:12], None, *refs[12:])
+    out, _, _ = pl.pallas_call(
+        kernel,
         out_shape=(
             jax.ShapeDtypeStruct((n_tok, width), jnp.bfloat16),
-            jax.ShapeDtypeStruct((n_a, chips, 2, rows, COLS_A), jnp.bfloat16),
-            jax.ShapeDtypeStruct((n_b, chips, 2, rows_b, COLS_B), jnp.bfloat16),
+            jax.ShapeDtypeStruct((n_a, chips, 2, 2, rows, COLS), jnp.bfloat16),
+            jax.ShapeDtypeStruct((n_b, chips, 2, 2, rows_b // 4, COLS), jnp.bfloat16),
         ),
-        in_specs=[any_spec] * 3 + [vmem_spec] * 4,
+        in_specs=[any_spec] * 8 + [vmem_spec] * (len(operands) - 8),
         out_specs=(any_spec,) * 3,
         scratch_shapes=[
             pltpu.VMEM((n_tok, width), jnp.bfloat16),
             pltpu.VMEM((n_tok, width), jnp.bfloat16),
             pltpu.VMEM((n_heads + 2 * kv_heads, n_tok, head_dim), jnp.bfloat16),
-            pltpu.VMEM((n_tok, ff), jnp.bfloat16),
-            pltpu.VMEM((2, chips, 2, rows, COLS_A), jnp.bfloat16),
-            pltpu.VMEM((2, chips, 2, rows_b, COLS_B), jnp.bfloat16),
+            pltpu.VMEM((2, n_tok, ff // 2), jnp.bfloat16),
+            pltpu.VMEM((n_tok, COLS), jnp.float32),
+            pltpu.VMEM((2, chips, 2, 2, rows, COLS), jnp.bfloat16),
+            pltpu.VMEM((2, chips, 2, 2, rows_b // 4, COLS), jnp.bfloat16),
             pltpu.SemaphoreType.DMA((n_a, N_RECV)),
             pltpu.SemaphoreType.DMA((n_b, N_RECV)),
             pltpu.SemaphoreType.DMA((n_a,)),
@@ -417,10 +487,10 @@
         ],
         compiler_params=pltpu.CompilerParams(
             collective_id=0, has_side_effects=True, vmem_limit_bytes=66_000_000),
-        cost_estimate=pl.CostEstimate(flops=flops, bytes_accessed=4 * n_dev * (w_a.size + w_b.size), transcendentals=0),
+        cost_estimate=pl.CostEstimate(flops=2 * n_tok * n_weights, bytes_accessed=4 * n_weights, transcendentals=0),
         name='prefill_layer',
-    )(h0.reshape(n_tok, width), w_a, w_b, cos, sin, gain_attn[None], gain_mlp[None])
-    return h_out.reshape(n_seq, seq_len, width)
+    )(*operands)
+    return out.reshape(n_seq, seq_len, width)
 
 
 def solution(mesh):
@@ -434,9 +504,10 @@
     def local_forward(h0, positions, norm_attn, norm_mlp, w_query, w_key, w_value, w_out, w_gate, w_up, w_down, norm_final):
         cos, sin = rope_tables(positions.reshape(-1), w_query.shape[-1])
         residual = h0
-        for l in range(w_query.shape[0]):
-            residual = run_layer(residual, cos, sin, norm_attn[l], norm_mlp[l], w_query[l], w_key[l], w_value[l],
-                                 w_out[l], w_gate[l], w_up[l], w_down[l], n_dev)
-        return rms_norm(residual, norm_final)
+        n_layers = w_query.shape[0]
+        for l in range(n_layers):
+            residual = run_layer(residual, cos, sin, norm_attn[l], norm_mlp[l], norm_final if l == n_layers - 1 else None,
+                                 w_query[l], w_key[l], w_value[l], w_out[l], w_gate[l], w_up[l], w_down[l], n_dev)
+        return residual
 
     return jax.shard_map(local_forward, mesh=mesh, in_specs=in_specs, out_specs=token_spec, check_vma=False)

time: 607 us -> 584 us (0.962)
  other arithmetic: 19.5 us -> 3.74 us
  local copies, waits for them, and re-layouts: 19.6 us -> 9.75 us
    convert_element_type x1 -> x0, other arithmetic: 8.02 us -> none  [rms_norm(): return (as_f32 * lax.rsqrt(mean_sq + EPS) * gain_vec).astype(jnp.bfloat16)]
    another operation x5 -> x1, local copies, waits for them, and re-layouts: 8.41 us -> 1.83 us  [run_layer(): w_q, w_k, w_v = (w.reshape(rows, -1) for w in (w_query, w_key, w_value))]
where the time goes in v2:
time: 584 us; the launch traced here: 583 us
  Pallas kernels  570 us (98%)
  local copies, waits for them, and re-layouts  9.75 us (2%)
    pallas_call x1, Pallas kernels, run_layer(): pl.pallas_call(kernel, out_shape=(jax.ShapeDtypeStruct((n_tok, width), jn...  570 us

profile of v2, /device:TPU:97, one launch (start us, length us, event | category | flops | bytes accessed | tf_op | source)
XLA Modules:
  0.0 583.4 jit_solution(13788169219716883489)
XLA Ops:
  0.0 0.7 convert_bitcast_fusion
  0.7 1.8 copy_bitcast_fusion.1
  2.5 2.0 copy.20
  4.5 3.0 fusion
  7.6 569.9 %prefill_layer.1 = (bf16[1024,3072]{1,0:T(8,128)(2,1)}, bf16[48,16,2,2,96,256]{5,4,3,2,1,0:T(8,128)(2,1)}, bf16[24,16,2,2,64,256]{5,4,3,2,1,0:T(8,128)(2,1)}) custom-call(bf16[1024,3072]{1,0:T(8,128)(2,1)} %bitcast.29, bf16[96,3072]{1,0:T(8,128)(2,1)} %bitcast.25, bf16[96,1024]{1,0:T(8,128)(2,1)} %get-tuple-element.12.w_k, ...), custom_call_target="tpu_custom_call" | custom-call | flops 206158430208 | bytes 402653184 | tf_op jit(solution)/shard_map/prefill_layer/pallas_call | solution.py:461
  577.5 5.9 %copy.22 = bf16[2,512,3072]{2,1,0:T(8,128)(2,1)} copy(bf16[2,512,3072]{2,1,0:T(8,128)(2,1)} %bitcast.23) | data formatting | bytes 12582912
  (2 shorter events, 0.0 us)

commit v3 on v2

--- a/solution.py
+++ b/solution.py
@@ -11,7 +11,9 @@
 EPS = 1e-5
 ROPE_BASE = 10000.0
 COLS = 256
-LAG = 5
+LAGS_A = (0, 2, 4, 6, 8, 9)
+LAGS_B = (0, 1, 2, 3, 4, 5)
+LAG_A, LAG_B = LAGS_A[-1], LAGS_B[-1]
 RING = 4
 N_RECV = 18
 MESH = pl.DeviceIdType.MESH
@@ -43,18 +45,18 @@
         self.core = lax.rem(me, 2)
         chip = me // 2
         col, row = lax.rem(chip, RING), chip // RING
-        core = self.core
-        self.chip = {}
-        for dp in (-1, 0, 1, 2):
-            for ds in (-1, 0, 1, 2):
-                cc = lax.rem(col + dp * (1 - core) + ds * core + RING, RING)
-                rr = lax.rem(row + dp * core + ds * (1 - core) + RING, RING)
-                self.chip[dp, ds] = rr * RING + cc
-        dev = lambda dp, ds: self.chip[dp, ds] * 2 + core
-        self.p_up, self.p_dn = dev(1, 0), dev(-1, 0)
-        self.s_up, self.s_dn = dev(0, 1), dev(0, -1)
-        self.twin = chip * 2 + 1 - core
+        at = lambda dc, dr: lax.rem(row + dr + RING, RING) * RING + lax.rem(col + dc + RING, RING)
+        self.at = {(i, j): at(i, j) for i in (-1, 0, 1, 2) for j in (-1, 0, 1, 2)}
+        self.near = tuple(self.at[rel] * 2 + self.core for rel in ((1, 0), (-1, 0), (0, 1), (0, -1)))
+        self.twin = chip * 2 + 1 - self.core
         self.me = me
+
+    def chip(self, blk, rel):
+        straight, turned = self.at[rel], self.at[rel[::-1]]
+        return straight + lax.rem(blk + self.core, 2) * (turned - straight)
+
+    def dev(self, blk, dp, ds):
+        return self.chip(blk, (dp, ds)) * 2 + self.core
 
 
 class Gather:
@@ -63,7 +65,7 @@
         self.recv, self.send_sem, self.twin_send = recv, send, twin_send
 
     def spot(self, blk, rel, part=None):
-        ref = self.full.at[blk, self.pl.chip[rel], self.pl.core]
+        ref = self.full.at[blk, self.pl.chip(blk, rel), self.pl.core]
         return ref if part is None else ref.at[part]
 
     def copy(self, blk, src, dst, r, dev):
@@ -81,7 +83,8 @@
 
     def first(self, blk, own):
         w = self.pl
-        for r, dev in ((R_M0, w.p_up), (R_P0, w.p_dn), (R_0M, w.s_up), (R_0P, w.s_dn)):
+        for r, rel in ((R_M0, (1, 0)), (R_P0, (-1, 0)), (R_0M, (0, 1)), (R_0P, (0, -1))):
+            dev = w.dev(blk, *rel)
             for part in range(2):
                 self.copy(blk, own(blk, part), self.spot(blk, (0, 0), part), r, dev).start()
         for part in range(2):
@@ -97,9 +100,10 @@
             src_ref=ref, dst_ref=ref, send_sem=self.twin_send.at[blk],
             recv_sem=self.recv.at[blk, R_TWIN], device_id={'wg': self.pl.twin}, device_id_type=MESH)
 
-    def stage(self, lag, blk):
+    def stage(self, step, blk):
         w, got, put = self.pl, self.got, self.put
-        if lag == 0:
+        p_up, p_dn, s_up, s_dn = (w.dev(blk, *rel) for rel in ((1, 0), (-1, 0), (0, 1), (0, -1)))
+        if step == 0:
             for lo, hi, own in self.own:
                 if lo == hi:
                     continue
@@ -109,30 +113,30 @@
                     @pl.when(jnp.logical_and(blk >= lo, blk < hi))
                     def _():
                         self.first(blk, own)
-        elif lag == 1:
+        elif step == 1:
             got(blk, (-1, 0), R_M0)
-            put(blk, (-1, 0), R_2A, w.p_up, 0)
-            put(blk, (-1, 0), R_MM, w.s_up)
-            put(blk, (-1, 0), R_MP, w.s_dn)
+            put(blk, (-1, 0), R_2A, p_up, 0)
+            put(blk, (-1, 0), R_MM, s_up)
+            put(blk, (-1, 0), R_MP, s_dn)
             got(blk, (1, 0), R_P0)
-            put(blk, (1, 0), R_2B, w.p_dn, 1)
-            put(blk, (1, 0), R_PM, w.s_up)
-            put(blk, (1, 0), R_PP, w.s_dn)
+            put(blk, (1, 0), R_2B, p_dn, 1)
+            put(blk, (1, 0), R_PM, s_up)
+            put(blk, (1, 0), R_PP, s_dn)
             got(blk, (0, -1), R_0M)
-            put(blk, (0, -1), R_0N, w.s_up)
-        elif lag == 2:
+            put(blk, (0, -1), R_0N, s_up)
+        elif step == 2:
             got(blk, (2, 0), R_2A, 0)
             got(blk, (2, 0), R_2B, 1)
-            put(blk, (2, 0), R_2M, w.s_up)
-            put(blk, (2, 0), R_2P, w.s_dn)
+            put(blk, (2, 0), R_2M, s_up)
+            put(blk, (2, 0), R_2P, s_dn)
             got(blk, (-1, -1), R_MM)
-            put(blk, (-1, -1), R_MN, w.s_up)
+            put(blk, (-1, -1), R_MN, s_up)
             got(blk, (1, 1), R_PP)
-            put(blk, (1, 1), R_P2, w.s_dn)
-        elif lag == 3:
+            put(blk, (1, 1), R_P2, s_dn)
+        elif step == 3:
             got(blk, (2, 1), R_2P)
-            put(blk, (2, 1), R_22, w.s_dn)
-        elif lag == 4:
+            put(blk, (2, 1), R_22, s_dn)
+        elif step == 4:
             for rel, r in (((1, -1), R_PM), ((2, -1), R_2M), ((0, 1), R_0P), ((-1, 1), R_MP),
                            ((0, 2), R_0N), ((-1, 2), R_MN), ((1, 2), R_P2), ((2, 2), R_22)):
                 got(blk, rel, r)
@@ -147,7 +151,7 @@
         self.twin_copy(blk, self.pl.core).wait_send()
 
 
-def layer_kernel(dims, h0, w_q, w_k, w_v, w_o, w_g, w_u, w_d, cos, sin, gain_attn, gain_mlp, gain_out, out_ref, full_a, full_b,
+def layer_kernel(dims, h0, w_q, w_k, w_v, w_o, w_g, w_u, w_d, cos, sin, gain_attn, gain_mlp, out_ref, full_a, full_b,
                  h_s, a_s, heads, u_s, acc_s, buf_a, buf_b, recv_a, recv_b, send_a, send_b, twin_a, twin_b, load_a, load_b, io_sem):
     n_seq, seq_len, n_heads, kv_heads, head_dim = dims
     n_tok, width = h_s.shape
@@ -184,22 +188,21 @@
     gb = Gather(place, [(0, n_b, down_part)], full_b, recv_b, send_b, twin_b)
 
     barrier = pltpu.get_barrier_semaphore()
-    near = (place.p_up, place.p_dn, place.s_up, place.s_dn, place.twin)
+    near = place.near + (place.twin,)
     for dev in near:
         pl.semaphore_signal(barrier, inc=1, device_id={'wg': dev}, device_id_type=MESH)
     pl.semaphore_wait(barrier, len(near))
 
     def tick(t, may_a=True, may_b=True):
-        for lag in range(LAG + 1):
-            blk = t - lag
+        for step, (lag_a, lag_b) in enumerate(zip(LAGS_A, LAGS_B)):
             if may_a:
-                @pl.when(jnp.logical_and(blk >= 0, blk < n_a))
+                @pl.when(jnp.logical_and(t - lag_a >= 0, t - lag_a < n_a))
                 def _():
-                    ga.stage(lag, blk)
+                    ga.stage(step, t - lag_a)
             if may_b:
-                @pl.when(jnp.logical_and(blk >= n_a, blk < n_a + n_b))
+                @pl.when(jnp.logical_and(t - lag_b >= n_a, t - lag_b < n_a + n_b))
                 def _():
-                    gb.stage(lag, blk - n_a)
+                    gb.stage(step, t - lag_b - n_a)
 
     def load_copy_a(i):
         slot = lax.rem(i, 2)
@@ -326,9 +329,17 @@
         def _():
             over_seqs(first_half)
 
+            @pl.when(i > 0)
+            def _():
+                put_out(i // 2 - 1)
+
         @pl.when(lax.rem(i, 2) == 1)
         def _():
             over_seqs(second_half)
+
+    def put_out(j):
+        cols = pl.ds(pl.multiple_of(j * COLS, COLS), COLS)
+        pltpu.make_async_copy(h_s.at[:, cols], out_ref.at[:, cols], io_sem.at[1]).start()
 
     def loop(lo, hi, body):
         def step(i, _):
@@ -344,22 +355,22 @@
     only_a(1)
     h_in.wait()
     now = 2
-    share = -(-n_norm // (LAG + 1 - now))
+    share = -(-n_norm // (LAG_A + 1 - now))
 
     def seg_start(i):
         only_a(i)
-        norm_into(gain_attn, (i - 2) * share, jnp.minimum((i - 1) * share, n_norm))
-    assert n_a > LAG + 1 + n_qk + n_v + n_seq * kv_heads // 2 + n_wo
-    loop(now, LAG + 1, seg_start)
-    now = LAG + 1
+        norm_into(gain_attn, jnp.minimum((i - 2) * share, n_norm), jnp.minimum((i - 1) * share, n_norm))
+    assert n_a > LAG_A + 1 + n_qk + n_v + n_seq * kv_heads // 2 + n_wo
+    loop(now, LAG_A + 1, seg_start)
+    now = LAG_A + 1
     load_copy_a(0).start()
 
     def seg_qk(i):
-        only_a(i + LAG + 1)
+        only_a(i + LAG_A + 1)
         project(i, True)
 
     def seg_v(i):
-        only_a(i + LAG + 1)
+        only_a(i + LAG_A + 1)
         project(i, False)
     loop(0, n_qk, seg_qk)
     loop(n_qk, n_qk + n_v, seg_v)
@@ -382,7 +393,7 @@
     now += n_wo
     norm_into(gain_mlp, 0, n_norm)
     rounds = n_gu // 4
-    need = max(first_gu + 4 * i + 4 + LAG - (3 * i + 2) for i in range(rounds))
+    need = max(first_gu + 4 * i + 4 + LAG_A - (3 * i + 2) for i in range(rounds))
     if now < need:
         loop(now, need, tick)
         now = need
@@ -399,47 +410,52 @@
         gate_up(4 * i + 3)
     loop(0, rounds, seg_gu)
     now += 3 * rounds
-    need = n_a + LAG + 1
+    need = n_a + max(LAG_A, LAG_B + 1)
     if now < need:
         loop(now, need, tick)
         now = need
-    down_from = now
-    late = functools.partial(tick, may_a=down_from < n_a + LAG)
-
-    def seg_down(i):
-        late(down_from + i)
-        down(i)
-    loop(0, n_b, seg_down)
-
-    if gain_out is None:
-        out_copy = pltpu.make_async_copy(h_s, out_ref, io_sem.at[1])
-        out_copy.start()
-    else:
-        def finish(i):
-            sl = pl.ds(pl.multiple_of(i * norm_rows, norm_rows), norm_rows)
-            a_s[sl, :] = rms_norm(h_s[sl, :], gain_out[...])
-
-            @pl.when(i > 0)
-            def _():
-                put_out(i - 1)
-
-        def put_out(i):
-            sl = pl.ds(pl.multiple_of(i * norm_rows, norm_rows), norm_rows)
-            pltpu.make_async_copy(a_s.at[sl], out_ref.at[sl], io_sem.at[1]).start()
-        loop(0, n_norm, finish)
-        out_copy = pltpu.make_async_copy(a_s, out_ref, io_sem.at[1])
+    only_b = functools.partial(tick, may_a=False)
+    pairs = min(now - n_a - LAG_B - 1, n_b // 2)
+    pair_from, one_from = now, now + pairs
+
+    def seg_pair(i):
+        only_b(pair_from + i)
+        down(2 * i)
+        down(2 * i + 1)
+    loop(0, pairs, seg_pair)
+
+    def seg_one(i):
+        only_b(one_from + i)
+        down(2 * pairs + i)
+    loop(0, n_b - 2 * pairs, seg_one)
+    assert one_from + n_b - 2 * pairs >= n_a + n_b + LAG_B
+
     loop(0, n_a, ga.drain)
     loop(0, n_b, gb.drain)
-    if gain_out is not None:
-        put_out(n_norm - 1)
-    out_copy.wait()
-
-
-def run_layer(h0, cos, sin, gain_attn, gain_mlp, gain_out, w_query, w_key, w_value, w_out, w_gate, w_up, w_down, n_dev):
-    n_seq, seq_len, width = h0.shape
+    put_out(n_b // 2 - 1)
+    pltpu.make_async_copy(h_s, out_ref, io_sem.at[1]).wait()
+
+
+def norm_kernel(h_ref, gain, out_ref):
+    out_ref[...] = rms_norm(h_ref[...], gain[...])
+
+
+def final_norm(h, gain):
+    n_tok, width = h.shape
+    rows = min(128, n_tok)
+    spec = pl.BlockSpec((rows, width), lambda i: (i, 0))
+    return pl.pallas_call(
+        norm_kernel, grid=(n_tok // rows,), in_specs=[spec, pl.BlockSpec((1, width), lambda i: (0, 0))], out_specs=spec,
+        out_shape=jax.ShapeDtypeStruct((n_tok, width), jnp.bfloat16), name='final_norm',
+        cost_estimate=pl.CostEstimate(flops=6 * n_tok * width, bytes_accessed=4 * n_tok * width, transcendentals=n_tok),
+    )(h, gain[None])
+
+
+def run_layer(h0, cos, sin, gain_attn, gain_mlp, w_query, w_key, w_value, w_out, w_gate, w_up, w_down, n_dev, n_seq):
+    n_tok, width = h0.shape
     rows, n_heads, head_dim = w_query.shape
     kv_heads = w_key.shape[1]
-    n_tok = n_seq * seq_len
+    seq_len = n_tok // n_seq
     ff = w_gate.shape[1]
     rows_b = w_down.shape[0]
     w_q, w_k, w_v = (w.reshape(rows, -1) for w in (w_query, w_key, w_value))
@@ -449,17 +465,9 @@
     any_spec = pl.BlockSpec(memory_space=pl.ANY)
     vmem_spec = pl.BlockSpec(memory_space=pltpu.VMEM)
     n_weights = n_dev * (n_a * rows * 2 * COLS + rows_b * width)
-    last = gain_out is not None
-    body = functools.partial(layer_kernel, (n_seq, seq_len, n_heads, kv_heads, head_dim))
-    operands = [h0.reshape(n_tok, width), w_q, w_k, w_v, w_out, w_gate, w_up, w_down, cos, sin, gain_attn[None], gain_mlp[None]]
-    if last:
-        operands.append(gain_out[None])
-        kernel = body
-    else:
-        def kernel(*refs):
-            return body(*refs[:12], None, *refs[12:])
+    operands = (h0, w_q, w_k, w_v, w_out, w_gate, w_up, w_down, cos, sin, gain_attn[None], gain_mlp[None])
     out, _, _ = pl.pallas_call(
-        kernel,
+        functools.partial(layer_kernel, (n_seq, seq_len, n_heads, kv_heads, head_dim)),
         out_shape=(
             jax.ShapeDtypeStruct((n_tok, width), jnp.bfloat16),
             jax.ShapeDtypeStruct((n_a, chips, 2, 2, rows, COLS), jnp.bfloat16),
@@ -490,7 +498,7 @@
         cost_estimate=pl.CostEstimate(flops=2 * n_tok * n_weights, bytes_accessed=4 * n_weights, transcendentals=0),
         name='prefill_layer',
     )(*operands)
-    return out.reshape(n_seq, seq_len, width)
+    return out
 
 
 def solution(mesh):
@@ -503,11 +511,10 @@
 
     def local_forward(h0, positions, norm_attn, norm_mlp, w_query, w_key, w_value, w_out, w_gate, w_up, w_down, norm_final):
         cos, sin = rope_tables(positions.reshape(-1), w_query.shape[-1])
-        residual = h0
-        n_layers = w_query.shape[0]
-        for l in range(n_layers):
-            residual = run_layer(residual, cos, sin, norm_attn[l], norm_mlp[l], norm_final if l == n_layers - 1 else None,
-                                 w_query[l], w_key[l], w_value[l], w_out[l], w_gate[l], w_up[l], w_down[l], n_dev)
-        return residual
+        residual = h0.reshape(-1, h0.shape[-1])
+        for l in range(w_query.shape[0]):
+            residual = run_layer(residual, cos, sin, norm_attn[l], norm_mlp[l], w_query[l], w_key[l], w_value[l],
+                                 w_out[l], w_gate[l], w_up[l], w_down[l], n_dev, h0.shape[0])
+        return final_norm(residual, norm_final).reshape(h0.shape)
 
     return jax.shard_map(local_forward, mesh=mesh, in_specs=in_specs, out_specs=token_spec, check_vma=False)

time: 584 us -> 570 us (0.976)
  Pallas kernels: 570 us -> 562 us
  local copies, waits for them, and re-layouts: 9.75 us -> 3.82 us
    pallas_call x1 -> x2, Pallas kernels: 570 us -> 562 us  [the longest x1 553 us: run_layer(): pl.pallas_call(functools.partial(layer_kernel, (n_seq, seq_len, n_heads,...]
    unnamed x3 -> x2, local copies, waits for them, and re-layouts: 7.92 us -> 1.99 us
where the time goes in v3:
time: 570 us
  Pallas kernels  562 us (99%)
    pallas_call x1, Pallas kernels, run_layer(): pl.pallas_call(functools.partial(layer_kernel, (n_seq, seq_len, n_heads,...  553 us

profile of v3, /device:TPU:97, one launch (start us, length us, event | category | flops | bytes accessed | tf_op | source)
XLA Modules:
  0.0 569.8 jit_solution(16130795677770469129)
XLA Ops:
  0.0 0.7 convert_bitcast_fusion
  0.7 1.8 copy_bitcast_fusion.1
  2.5 2.0 copy.20
  4.5 3.0 fusion
  7.6 553.2 %prefill_layer.1 = (bf16[1024,3072]{1,0:T(8,128)(2,1)}, bf16[48,16,2,2,96,256]{5,4,3,2,1,0:T(8,128)(2,1)}, bf16[24,16,2,2,64,256]{5,4,3,2,1,0:T(8,128)(2,1)}) custom-call(bf16[1024,3072]{1,0:T(8,128)(2,1)} %bitcast.29, bf16[96,3072]{1,0:T(8,128)(2,1)} %bitcast.24, bf16[96,1024]{1,0:T(8,128)(2,1)} %get-tuple-element.12.w_k, ...), custom_call_target="tpu_custom_call" | custom-call | flops 206158430208 | bytes 402653184 | tf_op jit(solution)/shard_map/prefill_layer/pallas_call | solution.py:469
  560.8 9.0 %final_norm.1 = bf16[1024,3072]{1,0:T(8,128)(2,1)} custom-call(bf16[1024,3072]{1,0:T(8,128)(2,1)} %get-tuple-element.6.h_ref, f32[1,3072]{1,0:T(1,128)} %bitcast.28), custom_call_target="tpu_custom_call" | custom-call | flops 18874368 | bytes 12582912 | tf_op jit(solution)/shard_map/final_norm/pallas_call | solution.py:447
  (2 shorter events, 0.0 us)

commit v4 on v3

--- a/solution.py
+++ b/solution.py
@@ -15,13 +15,12 @@
 LAGS_B = (0, 1, 2, 3, 4, 5)
 LAG_A, LAG_B = LAGS_A[-1], LAGS_B[-1]
 RING = 4
-N_RECV = 18
+AHEAD = 3
 MESH = pl.DeviceIdType.MESH
 
-R_M0, R_P0, R_2A, R_2B = 0, 1, 2, 3
-R_0M, R_MM, R_PM, R_2M, R_0N, R_MN = 4, 5, 6, 7, 8, 9
-R_0P, R_MP, R_PP, R_2P, R_P2, R_22 = 10, 11, 12, 13, 14, 15
-R_TWIN, R_OWN = 16, 17
+R_M0, R_P0, R_20, R_0M, R_MM, R_PP, R_2P, R_REST, R_TWIN, R_OWN = range(10)
+N_RECV = 10
+N_REST = 8
 
 
 def rms_norm(values_in, gain_vec):
@@ -32,11 +31,13 @@
 
 def rope_tables(positions, head_dim):
     half_dim = head_dim // 2
+    n_seq, seq_len = positions.shape
     lane = jnp.arange(head_dim)
     exponents = (lane % half_dim).astype(jnp.float32) * (2.0 / head_dim)
     inv_freq = jnp.power(jnp.float32(ROPE_BASE), -exponents)
-    angles = positions.astype(jnp.float32)[..., None] * inv_freq
-    return jnp.cos(angles), jnp.where(lane < half_dim, -1.0, 1.0) * jnp.sin(angles)
+    pairs = positions.astype(jnp.float32).reshape(n_seq // 2, 2, seq_len, 1)
+    angles = jnp.where(lane < half_dim, pairs[:, 0], pairs[:, 1]) * inv_freq
+    return tuple(f(angles).reshape(-1, head_dim) for f in (jnp.cos, jnp.sin))
 
 
 class Place:
@@ -81,18 +82,19 @@
         ref = self.spot(blk, rel, part)
         self.copy(blk, ref, ref, r, self.pl.me).wait_recv()
 
-    def first(self, blk, own):
-        w = self.pl
-        for r, rel in ((R_M0, (1, 0)), (R_P0, (-1, 0)), (R_0M, (0, 1)), (R_0P, (0, -1))):
-            dev = w.dev(blk, *rel)
-            for part in range(2):
-                self.copy(blk, own(blk, part), self.spot(blk, (0, 0), part), r, dev).start()
-        for part in range(2):
-            pltpu.make_async_copy(own(blk, part), self.spot(blk, (0, 0), part), self.recv.at[blk, R_OWN]).start()
-
-    def own_wait(self, blk):
-        ref = self.spot(blk, (0, 0))
-        pltpu.make_async_copy(ref, ref, self.recv.at[blk, R_OWN]).wait()
+    def place_own(self, blk):
+        for lo, hi, own in self.own:
+            def start():
+                for part in range(2):
+                    pltpu.make_async_copy(own(blk, part), self.spot(blk, (0, 0), part), self.recv.at[blk, R_OWN]).start()
+            if len(self.own) == 1:
+                start()
+            elif lo < hi:
+                pl.when(jnp.logical_and(blk >= lo, blk < hi))(start)
+
+    def take(self, blk, r, n_chunks):
+        ref = self.full.at[blk, pl.ds(0, n_chunks), 0]
+        pltpu.make_async_copy(ref, ref, self.recv.at[blk, r]).wait()
 
     def twin_copy(self, blk, core):
         ref = self.full.at[blk, :, core]
@@ -103,44 +105,37 @@
     def stage(self, step, blk):
         w, got, put = self.pl, self.got, self.put
         p_up, p_dn, s_up, s_dn = (w.dev(blk, *rel) for rel in ((1, 0), (-1, 0), (0, 1), (0, -1)))
+        own = (0, 0)
         if step == 0:
-            for lo, hi, own in self.own:
-                if lo == hi:
-                    continue
-                if len(self.own) == 1:
-                    self.first(blk, own)
-                else:
-                    @pl.when(jnp.logical_and(blk >= lo, blk < hi))
-                    def _():
-                        self.first(blk, own)
+            self.take(blk, R_OWN, 1)
+            put(blk, own, R_M0, p_up)
+            put(blk, own, R_P0, p_dn)
+            put(blk, own, R_0M, s_up)
+            put(blk, own, R_REST, s_dn)
         elif step == 1:
             got(blk, (-1, 0), R_M0)
-            put(blk, (-1, 0), R_2A, p_up, 0)
+            put(blk, (-1, 0), R_20, p_up, 0)
             put(blk, (-1, 0), R_MM, s_up)
-            put(blk, (-1, 0), R_MP, s_dn)
+            put(blk, (-1, 0), R_REST, s_dn)
             got(blk, (1, 0), R_P0)
-            put(blk, (1, 0), R_2B, p_dn, 1)
-            put(blk, (1, 0), R_PM, s_up)
+            put(blk, (1, 0), R_20, p_dn, 1)
+            put(blk, (1, 0), R_REST, s_up)
             put(blk, (1, 0), R_PP, s_dn)
             got(blk, (0, -1), R_0M)
-            put(blk, (0, -1), R_0N, s_up)
+            put(blk, (0, -1), R_REST, s_up)
         elif step == 2:
-            got(blk, (2, 0), R_2A, 0)
-            got(blk, (2, 0), R_2B, 1)
-            put(blk, (2, 0), R_2M, s_up)
+            got(blk, (2, 0), R_20)
+            put(blk, (2, 0), R_REST, s_up)
             put(blk, (2, 0), R_2P, s_dn)
             got(blk, (-1, -1), R_MM)
-            put(blk, (-1, -1), R_MN, s_up)
+            put(blk, (-1, -1), R_REST, s_up)
             got(blk, (1, 1), R_PP)
-            put(blk, (1, 1), R_P2, s_dn)
+            put(blk, (1, 1), R_REST, s_dn)
         elif step == 3:
             got(blk, (2, 1), R_2P)
-            put(blk, (2, 1), R_22, s_dn)
+            put(blk, (2, 1), R_REST, s_dn)
         elif step == 4:
-            for rel, r in (((1, -1), R_PM), ((2, -1), R_2M), ((0, 1), R_0P), ((-1, 1), R_MP),
-                           ((0, 2), R_0N), ((-1, 2), R_MN), ((1, 2), R_P2), ((2, 2), R_22)):
-                got(blk, rel, r)
-            self.own_wait(blk)
+            self.take(blk, R_REST, N_REST)
             self.twin_copy(blk, w.core).start()
         else:
             self.twin_copy(blk, 1 - w.core).wait_recv()
@@ -151,8 +146,8 @@
         self.twin_copy(blk, self.pl.core).wait_send()
 
 
-def layer_kernel(dims, h0, w_q, w_k, w_v, w_o, w_g, w_u, w_d, cos, sin, gain_attn, gain_mlp, out_ref, full_a, full_b,
-                 h_s, a_s, heads, u_s, acc_s, buf_a, buf_b, recv_a, recv_b, send_a, send_b, twin_a, twin_b, load_a, load_b, io_sem):
+def layer_kernel(dims, h0, w_q, w_k, w_v, w_o, w_g, w_u, w_d, cos2, sin2, gain_attn, gain_mlp, out_ref, full_a, full_b,
+                 h_s, a_s, heads, u_s, acc_s, cos, sin, buf_a, buf_b, recv_a, recv_b, send_a, send_b, twin_a, twin_b, load_a, load_b, io_sem):
     n_seq, seq_len, n_heads, kv_heads, head_dim = dims
     n_tok, width = h_s.shape
     n_rep = n_heads // kv_heads
@@ -187,13 +182,26 @@
     ga = Gather(place, own_a, full_a, recv_a, send_a, twin_a)
     gb = Gather(place, [(0, n_b, down_part)], full_b, recv_b, send_b, twin_b)
 
+    for blk in range(AHEAD):
+        ga.place_own(jnp.int32(blk))
     barrier = pltpu.get_barrier_semaphore()
     near = place.near + (place.twin,)
     for dev in near:
         pl.semaphore_signal(barrier, inc=1, device_id={'wg': dev}, device_id_type=MESH)
     pl.semaphore_wait(barrier, len(near))
 
+    def place_ahead(blk, may_a, may_b):
+        if may_a:
+            @pl.when(blk < n_a)
+            def _():
+                ga.place_own(blk)
+        if may_b:
+            @pl.when(jnp.logical_and(blk >= n_a, blk < n_a + n_b))
+            def _():
+                gb.place_own(blk - n_a)
+
     def tick(t, may_a=True, may_b=True):
+        place_ahead(t + AHEAD, may_a, may_b)
         for step, (lag_a, lag_b) in enumerate(zip(LAGS_A, LAGS_B)):
             if may_a:
                 @pl.when(jnp.logical_and(t - lag_a >= 0, t - lag_a < n_a))
@@ -357,6 +365,20 @@
     now = 2
     share = -(-n_norm // (LAG_A + 1 - now))
 
+    half_dim = head_dim // 2
+
+    def spread(i):
+        table = pl.ds(pl.multiple_of(i * seq_len, seq_len), seq_len)
+        low = lax.broadcasted_iota(jnp.int32, (seq_len, head_dim), 1) < half_dim
+        c, s = cos2[table, :], sin2[table, :]
+        c_turned, s_turned = pltpu.roll(c, half_dim, 1), pltpu.roll(s, half_dim, 1)
+        for j, (c_j, s_j) in enumerate(((jnp.where(low, c, c_turned), jnp.where(low, -s, s_turned)),
+                                        (jnp.where(low, c_turned, c), jnp.where(low, -s_turned, s)))):
+            rows = pl.ds(pl.multiple_of((2 * i + j) * seq_len, seq_len), seq_len)
+            cos[rows, :] = c_j
+            sin[rows, :] = s_j
+    loop(0, n_seq // 2, spread)
+
     def seg_start(i):
         only_a(i)
         norm_into(gain_attn, jnp.minimum((i - 2) * share, n_norm), jnp.minimum((i - 1) * share, n_norm))
@@ -423,6 +445,7 @@
         down(2 * i)
         down(2 * i + 1)
     loop(0, pairs, seg_pair)
+    loop(0, n_a, ga.drain)
 
     def seg_one(i):
         only_b(one_from + i)
@@ -430,7 +453,6 @@
     loop(0, n_b - 2 * pairs, seg_one)
     assert one_from + n_b - 2 * pairs >= n_a + n_b + LAG_B
 
-    loop(0, n_a, ga.drain)
     loop(0, n_b, gb.drain)
     put_out(n_b // 2 - 1)
     pltpu.make_async_copy(h_s, out_ref, io_sem.at[1]).wait()
@@ -481,6 +503,8 @@
             pltpu.VMEM((n_heads + 2 * kv_heads, n_tok, head_dim), jnp.bfloat16),
             pltpu.VMEM((2, n_tok, ff // 2), jnp.bfloat16),
             pltpu.VMEM((n_tok, COLS), jnp.float32),
+            pltpu.VMEM((n_tok, head_dim), jnp.float32),
+            pltpu.VMEM((n_tok, head_dim), jnp.float32),
             pltpu.VMEM((2, chips, 2, 2, rows, COLS), jnp.bfloat16),
             pltpu.VMEM((2, chips, 2, 2, rows_b // 4, COLS), jnp.bfloat16),
             pltpu.SemaphoreType.DMA((n_a, N_RECV)),
@@ -510,7 +534,7 @@
     assert n_dev == 2 * RING * RING
 
     def local_forward(h0, positions, norm_attn, norm_mlp, w_query, w_key, w_value, w_out, w_gate, w_up, w_down, norm_final):
-        cos, sin = rope_tables(positions.reshape(-1), w_query.shape[-1])
+        cos, sin = rope_tables(positions, w_query.shape[-1])
         residual = h0.reshape(-1, h0.shape[-1])
         for l in range(w_query.shape[0]):
             residual = run_layer(residual, cos, sin, norm_attn[l], norm_mlp[l], w_query[l], w_key[l], w_value[l],

time: 570 us -> 568 us (level)
  no operation moved by 1% of the time
where the time goes in v4:
time: 568 us; the launch traced here: 567 us
  Pallas kernels  561 us (99%)
    pallas_call x1, Pallas kernels, run_layer(): pl.pallas_call(functools.partial(layer_kernel, (n_seq, seq_len, n_heads,...  552 us

profile of v4, /device:TPU:97, one launch (start us, length us, event | category | flops | bytes accessed | tf_op | source)
XLA Modules:
  0.0 567.2 jit_solution(11018853313874075016)
XLA Ops:
  0.0 0.7 convert_bitcast_fusion
  0.7 1.8 copy_bitcast_fusion.1
  2.6 1.8 fusion
  4.4 2.0 copy.19
  6.3 551.8 %prefill_layer.1 = (bf16[1024,3072]{1,0:T(8,128)(2,1)}, bf16[48,16,2,2,96,256]{5,4,3,2,1,0:T(8,128)(2,1)}, bf16[24,16,2,2,64,256]{5,4,3,2,1,0:T(8,128)(2,1)}) custom-call(bf16[1024,3072]{1,0:T(8,128)(2,1)} %bitcast.31, bf16[96,3072]{1,0:T(8,128)(2,1)} %bitcast.25, bf16[96,1024]{1,0:T(8,128)(2,1)} %get-tuple-element.12.w_k, ...), custom_call_target="tpu_custom_call" | custom-call | flops 206158430208 | bytes 402653184 | tf_op jit(solution)/shard_map/prefill_layer/pallas_call | solution.py:491
  558.2 9.0 %final_norm.1 = bf16[1024,3072]{1,0:T(8,128)(2,1)} custom-call(bf16[1024,3072]{1,0:T(8,128)(2,1)} %get-tuple-element.6.h_ref, f32[1,3072]{1,0:T(1,128)} %bitcast.28), custom_call_target="tpu_custom_call" | custom-call | flops 18874368 | bytes 12582912 | tf_op jit(solution)/shard_map/final_norm/pallas_call | solution.py:469
  (3 shorter events, 0.0 us)

commit v5 on v4

--- a/solution.py
+++ b/solution.py
@@ -12,7 +12,7 @@
 ROPE_BASE = 10000.0
 COLS = 256
 LAGS_A = (0, 2, 4, 6, 8, 9)
-LAGS_B = (0, 1, 2, 3, 4, 5)
+LAGS_B = (0, 1, 2, 3, 5, 6)
 LAG_A, LAG_B = LAGS_A[-1], LAGS_B[-1]
 RING = 4
 AHEAD = 3
@@ -458,17 +458,41 @@
     pltpu.make_async_copy(h_s, out_ref, io_sem.at[1]).wait()
 
 
-def norm_kernel(h_ref, gain, out_ref):
-    out_ref[...] = rms_norm(h_ref[...], gain[...])
+def norm_kernel(h_ref, gain, out_ref, h_s, out_s, in_sem, out_sem):
+    n_part, rows, _ = h_s.shape
+
+    def part_in(i):
+        return pltpu.make_async_copy(h_ref.at[pl.ds(i * rows, rows)], h_s.at[i], in_sem.at[i])
+
+    def part_out(i):
+        return pltpu.make_async_copy(out_s.at[i], out_ref.at[pl.ds(i * rows, rows)], out_sem.at[i])
+    for i in range(n_part):
+        part_in(i).start()
+    sub = min(64, rows)
+    for i in range(n_part):
+        part_in(i).wait()
+
+        def body(j, _):
+            sl = pl.ds(pl.multiple_of(j * sub, sub), sub)
+            out_s[i, sl, :] = rms_norm(h_s[i, sl, :], gain[...])
+            return 0
+        lax.fori_loop(0, rows // sub, body, 0)
+        part_out(i).start()
+    for i in range(n_part):
+        part_out(i).wait()
 
 
 def final_norm(h, gain):
     n_tok, width = h.shape
-    rows = min(128, n_tok)
-    spec = pl.BlockSpec((rows, width), lambda i: (i, 0))
+    n_part = 8
+    rows = n_tok // n_part
+    any_spec = pl.BlockSpec(memory_space=pl.ANY)
     return pl.pallas_call(
-        norm_kernel, grid=(n_tok // rows,), in_specs=[spec, pl.BlockSpec((1, width), lambda i: (0, 0))], out_specs=spec,
+        norm_kernel, in_specs=[any_spec, pl.BlockSpec(memory_space=pltpu.VMEM)], out_specs=any_spec,
         out_shape=jax.ShapeDtypeStruct((n_tok, width), jnp.bfloat16), name='final_norm',
+        scratch_shapes=[pltpu.VMEM((n_part, rows, width), jnp.bfloat16), pltpu.VMEM((n_part, rows, width), jnp.bfloat16),
+                        pltpu.SemaphoreType.DMA((n_part,)), pltpu.SemaphoreType.DMA((n_part,))],
+        compiler_params=pltpu.CompilerParams(vmem_limit_bytes=66_000_000),
         cost_estimate=pl.CostEstimate(flops=6 * n_tok * width, bytes_accessed=4 * n_tok * width, transcendentals=n_tok),
     )(h, gain[None])
 

time: 568 us -> 561 us (0.988)
  Pallas kernels: 561 us -> 555 us
where the time goes in v5:
time: 561 us
  Pallas kernels  555 us (99%)
    pallas_call x1, Pallas kernels, run_layer(): pl.pallas_call(functools.partial(layer_kernel, (n_seq, seq_len, n_heads,...  549 us

profile of v5, /device:TPU:97, one launch (start us, length us, event | category | flops | bytes accessed | tf_op | source)
XLA Modules:
  0.0 561.1 jit_solution(11338403590928275713)
XLA Ops:
  0.0 0.7 convert_bitcast_fusion
  0.7 1.8 copy_bitcast_fusion.1
  2.6 1.8 fusion
  4.4 2.0 copy.19
  6.3 548.8 %prefill_layer.1 = (bf16[1024,3072]{1,0:T(8,128)(2,1)}, bf16[48,16,2,2,96,256]{5,4,3,2,1,0:T(8,128)(2,1)}, bf16[24,16,2,2,64,256]{5,4,3,2,1,0:T(8,128)(2,1)}) custom-call(bf16[1024,3072]{1,0:T(8,128)(2,1)} %bitcast.31, bf16[96,3072]{1,0:T(8,128)(2,1)} %bitcast.25, bf16[96,1024]{1,0:T(8,128)(2,1)} %get-tuple-element.12.w_k, ...), custom_call_target="tpu_custom_call" | custom-call | flops 206158430208 | bytes 402653184 | tf_op jit(solution)/shard_map/prefill_layer/pallas_call | solution.py:515
  555.1 5.8 %final_norm.1 = bf16[1024,3072]{1,0:T(8,128)(2,1)} custom-call(bf16[1024,3072]{1,0:T(8,128)(2,1)} %get-tuple-element.6.h_ref, f32[1,3072]{1,0:T(1,128)} %bitcast.28), custom_call_target="tpu_custom_call" | custom-call | flops 18874368 | bytes 12582912 | tf_op jit(solution)/shard_map/final_norm/pallas_call | solution.py:490
  (3 shorter events, 0.0 us)
